TPU v7x, 512 devices: a whole 4x8x8 slice. The times are simulated.
512 devices in a mesh: dp: 16 (over z, core), rows: 32 (over y, x).
Axes of the slice: x: 4, y: 8, z: 8, core: 2. Of those that a mesh axis runs over, the one named last changes fastest.
Arguments:
- latent: bfloat16 [32, 32, 64, 640], P('dp', 'rows'), may hold values from -16.25 to 16.25
- hidden: bfloat16 [32, 32, 64, 640], P('dp', 'rows'), may hold values from -16.25 to 16.25
- cotangent: bfloat16 [32, 32, 64, 640], P('dp', 'rows'), may hold values from -6 to 6
- filter_one: bfloat16 [9, 640, 640], P(None, 'dp', 'rows'), may hold values from -0.078125 to 0.078125
- filter_two: bfloat16 [9, 640, 640], P(None, 'dp', 'rows'), may hold values from -0.078125 to 0.078125
- gain_one: float32 [640], replicated, may hold values from 0.1 to 1.9
- shift_one: float32 [640], replicated, may hold values from -2.5 to 2.5
- gain_two: float32 [640], replicated, may hold values from 0.1 to 1.9
- shift_two: float32 [640], replicated, may hold values from -2.5 to 2.5
Outputs:
- latent_grad: bfloat16 [32, 32, 64, 640], P('dp', 'rows')
All inputs are finite; a program needn't handle non-finite values.
Results may differ from a plain program's by a relative error of at most 0.0027.
Values may be sent and summed in bfloat16 or wider, within the bound.
A program may use at most 128 MiB of HBM per device.

v0:
```python
import jax
import jax.numpy as jnp
from jax import lax
from jax.sharding import PartitionSpec as P

GROUPS = 16
GSIZE = 40


def from_everyone(shard, axis):
    length = lax.axis_size(axis)
    return lax.all_to_all(
        jnp.broadcast_to(shard[None], (length, *shard.shape)), axis, 0, 0, tiled=True
    )


def of_everyone(shard, axis):
    return from_everyone(shard, axis).sum(axis=0)


def in_one(arrays, axis):
    ends = [0]
    for a in arrays:
        ends.append(ends[-1] + a.size)
    so_far = of_everyone(jnp.concatenate([a.ravel() for a in arrays]), axis)
    return tuple((so_far[b:e].reshape(a.shape) for a, b, e in zip(arrays, ends, ends[1:])))


def extended(block, sides, width):
    for axis, dim in sides:
        count = lax.axis_size(axis)
        forward = [(i, i + 1) for i in range(count - 1)]
        backward = [(target, source) for source, target in forward]
        low = lax.ppermute(
            lax.slice_in_dim(block, block.shape[dim] - width, None, axis=dim), axis, forward
        )
        high = lax.ppermute(lax.slice_in_dim(block, 0, width, axis=dim), axis, backward)
        block = jnp.concatenate([low, block, high], axis=dim)
    return block


def joined_along(tiles, dim):
    tiles = jnp.moveaxis(tiles, 0, dim)
    lengths = tiles.shape
    return tiles.reshape(*lengths[:dim], lengths[dim] * lengths[dim + 1], *lengths[dim + 2 :])


def gathered_copies(shard, axis, dim):
    return joined_along(from_everyone(shard, axis), dim)


def group_sums(values):
    per_channel = jnp.sum(values, axis=(1, 2))
    return jnp.sum(per_channel.reshape(per_channel.shape[0], GROUPS, -1), axis=2)


def expand_groups(moment):
    return jnp.repeat(moment, GSIZE, axis=1)[:, None, None, :]


def finish_stats(sum_plain, sum_square, number):
    average = sum_plain / number
    variance = sum_square / number - average * average
    return (average, lax.rsqrt(variance + 1e-05))


def norm_backward(field, stats, gain, shift, incoming, number):
    average, inverse = stats
    values = field.astype(jnp.float32)
    normed = (values - expand_groups(average)) * expand_groups(inverse)
    linear = normed * gain + shift
    logistic = jax.nn.sigmoid(linear)
    scaled = incoming * logistic * (1.0 + linear * (1.0 - logistic)) * gain
    sum_first, sum_second = in_one((group_sums(scaled), group_sums(scaled * normed)), "rows")
    first = sum_first / number
    second = sum_second / number
    return expand_groups(inverse) * (scaled - expand_groups(first) - normed * expand_groups(second))


def conv_backward(gradient, weights):
    images, rows_here, breadth, channels = gradient.shape
    padded = extended(gradient, (("rows", 1),), 1)
    padded = jnp.pad(padded, ((0, 0), (0, 0), (1, 1), (0, 0)))
    pixels = images * rows_here * breadth
    shifted = []
    for tap_index in range(9):
        down_step = tap_index // 3 - 1
        side_step = tap_index % 3 - 1
        window = padded[
            :, 1 - down_step : 1 - down_step + rows_here, 1 - side_step : 1 - side_step + breadth, :
        ]
        shifted.append(window.reshape(pixels, channels))
    stacked = jnp.stack(shifted, axis=1)
    gathered = gathered_copies(weights, "rows", 2)
    flat_windows = stacked.reshape(pixels, 9 * channels)
    section = lax.all_gather(gathered, "dp", axis=1, tiled=True)
    flat = jnp.transpose(section, (0, 2, 1)).reshape(9 * channels, section.shape[1])
    result = jnp.dot(flat_windows, flat, preferred_element_type=jnp.float32)
    return result.reshape(images, rows_here, breadth, channels)


def body(
    latent, hidden, cotangent, filter_one, filter_two, gain_one, shift_one, gain_two, shift_two
):
    number = latent.shape[1] * lax.axis_size("rows") * latent.shape[2] * GSIZE
    latent_values = latent.astype(jnp.float32)
    hidden_values = hidden.astype(jnp.float32)
    sum_latent, square_latent, sum_hidden, square_hidden = in_one(
        (
            group_sums(latent_values),
            group_sums(latent_values * latent_values),
            group_sums(hidden_values),
            group_sums(hidden_values * hidden_values),
        ),
        "rows",
    )
    stats_one = finish_stats(sum_latent, square_latent, number)
    stats_two = finish_stats(sum_hidden, square_hidden, number)
    back_two = conv_backward(cotangent, filter_two)
    hidden_grad = norm_backward(hidden, stats_two, gain_two, shift_two, back_two, number).astype(
        jnp.bfloat16
    )
    back_one = conv_backward(hidden_grad, filter_one)
    latent_part = norm_backward(latent, stats_one, gain_one, shift_one, back_one, number)
    return (cotangent.astype(jnp.float32) + latent_part).astype(jnp.bfloat16)


def solution(mesh):
    in_specs = (
        P("dp", "rows", None, None),
        P("dp", "rows", None, None),
        P("dp", "rows", None, None),
        P(None, "dp", "rows"),
        P(None, "dp", "rows"),
        P(),
        P(),
        P(),
        P(),
    )
    out_specs = P("dp", "rows", None, None)
    return jax.shard_map(body, mesh=mesh, in_specs=in_specs, out_specs=out_specs, check_vma=False)
```

profile of v0, /device:TPU:192, one launch (start us, length us, event | category | flops | bytes accessed | tf_op | source)
XLA Modules:
  0.0 237.9 jit_solution(1815870196631016417)
XLA Ops:
  6.5 0.8 copy-done
  7.3 0.2 broadcast_bitcast_fusion.1
  7.6 2.1 reshape.248
  9.7 26.6 %all_to_all.28 = bf16[32,2,3600]{2,1,0:T(2,128)(2,1)S(1)} all-to-all(bf16[32,2,3600]{2,1,0:T(2,128)(2,1)S(1)} %reshape.248), channel_id=1, replica_groups=mesh['dp'=16,'rows'=32] {'rows'}, dimensions={0} | all-to-all | bytes 921600 | tf_op jit(solution)/shard_map/all_to_all | solution.py:12
  36.2 2.2 reshape.249
  38.4 1.5 bitcast_bitcast_fusion.1
  39.9 6.1 %copy.133 = bf16[9,40,32,20]{3,2,1,0:T(8,128)(2,1)S(1)} copy(bf16[9,40,32,20]{1,3,0,2:T(8,128)(2,1)} %bitcast_bitcast_fusion.1) | data formatting | bytes 921600 | tf_op jit(solution)/shard_map/reshape | solution.py:45
  46.0 6.3 %reshape.246 = bf16[9,40,640]{2,1,0:T(8,128)(2,1)} reshape(bf16[9,40,32,20]{3,2,1,0:T(8,128)(2,1)S(1)} %copy.133) | data formatting | bytes 921600 | tf_op jit(solution)/shard_map/reshape | solution.py:45
  52.4 0.2 broadcast_bitcast_fusion
  52.7 2.1 reshape.250
  54.7 20.5 %all_to_all.29 = bf16[32,2,3600]{2,1,0:T(2,128)(2,1)S(1)} all-to-all(bf16[32,2,3600]{2,1,0:T(2,128)(2,1)S(1)} %reshape.250), channel_id=1, replica_groups=mesh['dp'=16,'rows'=32] {'rows'}, dimensions={0} | all-to-all | bytes 921600 | tf_op jit(solution)/shard_map/all_to_all | solution.py:12
  75.2 2.2 reshape.251
  77.4 1.5 bitcast_bitcast_fusion
  78.9 6.1 %copy.134 = bf16[9,40,32,20]{3,2,1,0:T(8,128)(2,1)S(1)} copy(bf16[9,40,32,20]{1,3,0,2:T(8,128)(2,1)} %bitcast_bitcast_fusion) | data formatting | bytes 921600 | tf_op jit(solution)/shard_map/reshape | solution.py:45
  85.1 6.3 %reshape.247 = bf16[9,40,640]{2,1,0:T(8,128)(2,1)} reshape(bf16[9,40,32,20]{3,2,1,0:T(8,128)(2,1)S(1)} %copy.134) | data formatting | bytes 921600 | tf_op jit(solution)/shard_map/reshape | solution.py:45
  92.7 0.6 broadcast_in_dim.26
  93.3 4.4 %all-to-all-start = ((f32[32,1,128]{2,1,0:T(1,128)}), f32[32,1,128]{2,1,0:T(1,128)S(1)}, u32[]{:S(2)}, u32[]{:S(2)}) async-start(f32[32,1,128]{2,1,0:T(1,128)} %broadcast_in_dim.26), calls=%async_computation | async-start | bytes 32768 | tf_op jit(solution)/shard_map/all_to_all | solution.py:12
  97.8 3.7 %collective-permute-start = (bf16[2,1,64,640]{3,2,1,0:T(8,128)(2,1)S(1)}, bf16[2,1,64,640]{3,2,1,0:T(8,128)(2,1)S(1)}, u32[]{:S(2)}, u32[]{:S(2)}) collective-permute-start(bf16[2,1,64,640]{3,2,1,0:T(8,128)(2,1)S(1)} %copy-done.2), channel_id=1, source_target_pairs={{0,1},{1,2},{2,3},{3,4},{4,5},{5,6},{6,7},{7,8},{8,9},{9,10},{10,1... | collective-permute-start | bytes 491528 | tf_op jit(solution)/shard_map/ppermute | solution.py:34
  101.5 1.3 collective-permute-start.1
  102.8 0.3 copy.110
  103.1 4.4 %all-to-all-done = f32[32,1,128]{2,1,0:T(1,128)S(1)} async-done(((f32[32,1,128]{2,1,0:T(1,128)}), f32[32,1,128]{2,1,0:T(1,128)S(1)}, u32[]{:S(2)}, u32[]{:S(2)}) %all-to-all-start) | async-done | bytes 16416 | tf_op jit(solution)/shard_map/all_to_all | solution.py:12
  107.8 0.1 mul.122
  108.0 0.1 sub.60
  108.1 0.6 collective-permute-done.1
  108.7 0.2 fusion.15
  108.9 0.2 fusion.55
  109.0 0.3 copy.106
  109.3 1.0 copy.108
  110.3 1.0 copy.109
  111.2 1.0 copy.111
  112.2 1.0 copy.112
  113.2 1.0 copy.114
  114.2 1.0 copy.107
  115.2 1.0 copy.113
  116.2 11.1 %stack.6 = bf16[128,9,640]{2,1,0:T(8,128)(2,1)S(1)} concatenate(bf16[128,1,640]{2,1,0:T(2,128)(2,1)S(1)} %copy.106, bf16[128,1,640]{2,1,0:T(2,128)(2,1)} %copy.107, bf16[128,1,640]{2,1,0:T(2,128)(2,1)} %copy.108, bf16[128,1,640]{2,1,0:T(2,128)(2,1)} %copy.109, bf16[128,1,640]{2,1,0:T(2,128)(2,1)S(1)} %copy.110, bf16[128,1,640]{2,1,0:T(2,128)(2,1)} %copy.111, ...), dimensions={1} | concatenate | bytes 2949120 | tf_op jit(solution)/shard_map/stack | solution.py:93
  127.2 1.8 reshape.230
  129.0 12.6 %copy.117 = bf16[9,640,640]{2,1,0:T(8,128)(2,1)} copy(bf16[9,640,640]{1,2,0:T(8,128)(2,1)} %bitcast.82) | data formatting | bytes 14745600 | tf_op jit(solution)/shard_map/transpose | solution.py:97
  141.6 4.7 %fusion.53 = (f32[2,640]{1,0:T(2,128)S(1)}, f32[2,640]{1,0:T(2,128)S(1)}, f32[2,1,64,640]{3,2,0,1:T(8,128)S(1)}) fusion(f32[2,640]{1,0:T(2,128)S(1)} %mul.122, f32[2,640]{1,0:T(2,128)S(1)} %sub.60, bf16[2,1,64,640]{3,2,1,0:T(8,128)(2,1)S(1)} %copy-done.7, f32[640]{0:T(1024)S(1)} %copy-done.9, f32[640]{0:T(1024)S(1)} %copy-done.10, ...), kind=kOutput, calls=%fused_computation.78 | convolution fusion | flops 945108480 | bytes 9364480 | tf_op jit(solution)/shard_map/dot_general | solution.py:98
  146.9 0.6 broadcast_in_dim.31
  147.6 11.5 %all-to-all-start.2 = ((f32[32,1,64]{2,1,0:T(1,128)}), f32[32,1,64]{2,1,0:T(1,128)S(1)}, u32[]{:S(2)}, u32[]{:S(2)}) async-start(f32[32,1,64]{2,1,0:T(1,128)} %broadcast_in_dim.31), calls=%async_computation.2 | async-start | bytes 32768 | tf_op jit(solution)/shard_map/all_to_all | solution.py:12
  159.2 9.5 %all-to-all-done.2 = f32[32,1,64]{2,1,0:T(1,128)S(1)} async-done(((f32[32,1,64]{2,1,0:T(1,128)}), f32[32,1,64]{2,1,0:T(1,128)S(1)}, u32[]{:S(2)}, u32[]{:S(2)}) %all-to-all-start.2) | async-done | bytes 8224 | tf_op jit(solution)/shard_map/all_to_all | solution.py:12
  169.3 0.1 sub.64
  169.5 2.5 %collective-permute-start.2 = (bf16[2,1,64,640]{3,2,0,1:T(8,128)(2,1)S(1)}, bf16[2,1,64,640]{3,2,0,1:T(8,128)(2,1)S(1)}, u32[]{:S(2)}, u32[]{:S(2)}) collective-permute-start(bf16[2,1,64,640]{3,2,0,1:T(8,128)(2,1)S(1)} %fusion.50), channel_id=1, source_target_pairs={{0,1},{1,2},{2,3},{3,4},{4,5},{5,6},{6,7},{7,8},{8,9},{9,10},{10,1... | collective-permute-start | bytes 491528 | tf_op jit(solution)/shard_map/ppermute | solution.py:34
  172.0 1.5 collective-permute-start.3
  173.6 0.1 mul.119
  173.7 0.1 sub.68
  173.9 12.4 %copy.130 = bf16[9,640,640]{2,1,0:T(8,128)(2,1)} copy(bf16[9,640,640]{1,2,0:T(8,128)(2,1)} %bitcast.81) | data formatting | bytes 14745600 | tf_op jit(solution)/shard_map/transpose | solution.py:97
  186.2 0.3 copy.123
  186.5 0.2 fusion.17
  186.7 0.2 fusion.54
  186.8 0.3 copy.119
  187.1 1.0 copy.121
  188.1 1.0 copy.122
  189.1 1.0 copy.124
  190.0 1.0 copy.125
  191.0 1.0 copy.127
  192.0 1.0 copy.120
  193.0 1.0 copy.126
  194.0 11.0 %stack.7 = bf16[128,9,640]{2,1,0:T(8,128)(2,1)S(1)} concatenate(bf16[128,1,640]{2,1,0:T(2,128)(2,1)S(1)} %copy.119, bf16[128,1,640]{2,1,0:T(2,128)(2,1)} %copy.120, bf16[128,1,640]{2,1,0:T(2,128)(2,1)} %copy.121, bf16[128,1,640]{2,1,0:T(2,128)(2,1)} %copy.122, bf16[128,1,640]{2,1,0:T(2,128)(2,1)S(1)} %copy.123, bf16[128,1,640]{2,1,0:T(2,128)(2,1)} %copy.124, ...), dimensions={1} | concatenate | bytes 2949120 | tf_op jit(solution)/shard_map/stack | solution.py:93
  205.0 1.7 reshape.237
  206.8 5.0 %fusion.52 = (f32[2,640]{1,0:T(2,128)S(1)}, f32[2,640]{1,0:T(2,128)S(1)}, f32[2,1,64,640]{3,2,0,1:T(8,128)S(1)}) fusion(f32[2,640]{1,0:T(2,128)S(1)} %mul.119, f32[2,640]{1,0:T(2,128)S(1)} %sub.68, bf16[2,1,64,640]{3,2,1,0:T(8,128)(2,1)S(1)} %copy-done.5, f32[640]{0:T(1024)S(1)} %copy-done.11, f32[640]{0:T(1024)S(1)} %copy-done.12, ...), kind=kOutput, calls=%fused_computation.77 | convolution fusion | flops 945108480 | bytes 9364480 | tf_op jit(solution)/shard_map/dot_general | solution.py:98
  212.4 17.3 %all_to_all.30 = f32[32,1,64]{2,1,0:T(1,128)S(1)} all-to-all(f32[32,1,64]{2,1,0:T(1,128)S(1)} %broadcast_in_dim.72), channel_id=1, replica_groups=mesh['dp'=16,'rows'=32] {'rows'}, dimensions={0} | all-to-all | bytes 16384 | tf_op jit(solution)/shard_map/all_to_all | solution.py:12
  230.2 0.1 sub.72
  230.3 0.8 fusion.51
  (91 shorter events, 4.4 us)
Async XLA Ops:
  6.5 0.8 copy-start
  6.5 122.5 %all-gather.3.cloned.1.call-start = ((), (), s32[]{:S(2)}) async-start(), calls=%async_computation.5 | async-start | bytes 7833600 | tf_op jit(solution)/shard_map/all_gather | solution.py:96
  46.0 6.4 %copy-start.8 = (bf16[9,40,20]{1,2,0:T(8,128)(2,1)S(1)}, bf16[9,40,20]{1,2,0:T(8,128)(2,1)}, u32[]{:S(2)}) copy-start(bf16[9,40,20]{1,2,0:T(8,128)(2,1)} %param.12) | copy-start | bytes 43204
  52.4 121.5 %all-gather.5.cloned.1.call-start = ((), (), s32[]{:S(2)}) async-start(), calls=%async_computation.6 | async-start | bytes 7833600 | tf_op jit(solution)/shard_map/all_gather | solution.py:96
  85.0 6.4 %copy-start.4 = (bf16[2,1,64,640]{3,2,1,0:T(8,128)(2,1)S(1)}, bf16[2,1,64,640]{3,2,1,0:T(8,128)(2,1)}, u32[]{:S(2)}) copy-start(bf16[2,1,64,640]{3,2,1,0:T(8,128)(2,1)} %param.9) | copy-start | bytes 491524
  85.0 7.0 %copy-start.6 = (bf16[2,1,64,640]{3,2,1,0:T(8,128)(2,1)S(1)}, bf16[2,1,64,640]{3,2,1,0:T(8,128)(2,1)}, u32[]{:S(2)}) copy-start(bf16[2,1,64,640]{3,2,1,0:T(8,128)(2,1)} %param.10) | copy-start | bytes 491524
  85.0 12.7 %copy-start.2 = (bf16[2,1,64,640]{3,2,1,0:T(8,128)(2,1)S(1)}, bf16[2,1,64,640]{3,2,1,0:T(8,128)(2,1)}, u32[]{:S(2)}) copy-start(bf16[2,1,64,640]{3,2,1,0:T(8,128)(2,1)} %param.11) | copy-start | bytes 491524
  93.3 14.1 %all-to-all-start = ((f32[32,1,128]{2,1,0:T(1,128)}), f32[32,1,128]{2,1,0:T(1,128)S(1)}, u32[]{:S(2)}, u32[]{:S(2)}) async-start(f32[32,1,128]{2,1,0:T(1,128)} %broadcast_in_dim.26), calls=%async_computation | async-start | bytes 32768 | tf_op jit(solution)/shard_map/all_to_all | solution.py:12
  97.8 10.3 %collective-permute-start = (bf16[2,1,64,640]{3,2,1,0:T(8,128)(2,1)S(1)}, bf16[2,1,64,640]{3,2,1,0:T(8,128)(2,1)S(1)}, u32[]{:S(2)}, u32[]{:S(2)}) collective-permute-start(bf16[2,1,64,640]{3,2,1,0:T(8,128)(2,1)S(1)} %copy-done.2), channel_id=1, source_target_pairs={{0,1},{1,2},{2,3},{3,4},{4,5},{5,6},{6,7},{7,8},{8,9},{9,10},{10,1... | collective-permute-start | bytes 491528 | tf_op jit(solution)/shard_map/ppermute | solution.py:34
  101.5 7.2 %collective-permute-start.1 = (bf16[2,1,64,640]{3,2,1,0:T(8,128)(2,1)S(1)}, bf16[2,1,64,640]{3,2,1,0:T(8,128)(2,1)S(1)}, u32[]{:S(2)}, u32[]{:S(2)}) collective-permute-start(bf16[2,1,64,640]{3,2,1,0:T(8,128)(2,1)S(1)} %copy-done.2), channel_id=1, source_target_pairs={{1,0},{2,1},{3,2},{4,3},{5,4},{6,5},{7,6},{8,7},{9,8},{10,9},{11,1... | collective-permute-start | bytes 491528 | tf_op jit(solution)/shard_map/ppermute | solution.py:37
  129.0 12.6 %copy-start.3 = (bf16[2,64,5760]{2,1,0:T(8,128)(2,1)S(1)}, bf16[2,64,5760]{2,1,0:T(8,128)(2,1)}, u32[]{:S(2)}) copy-start(bf16[2,64,5760]{2,1,0:T(8,128)(2,1)} %reshape.230) | copy-start | bytes 4423684
  129.0 12.6 %copy-start.7 = (bf16[2,1,64,640]{3,2,1,0:T(8,128)(2,1)S(1)}, bf16[2,1,64,640]{3,2,1,0:T(8,128)(2,1)}, u32[]{:S(2)}) copy-start(bf16[2,1,64,640]{3,2,1,0:T(8,128)(2,1)} %param.10) | copy-start | bytes 491524
  129.0 12.6 %copy-start.9 = (f32[640]{0:T(1024)S(1)}, f32[640]{0:T(1024)}, u32[]{:S(2)}) copy-start(f32[640]{0:T(1024)} %param.17) | copy-start | bytes 7684
  129.0 12.6 %copy-start.10 = (f32[640]{0:T(1024)S(1)}, f32[640]{0:T(1024)}, u32[]{:S(2)}) copy-start(f32[640]{0:T(1024)} %param.16) | copy-start | bytes 7684
  147.6 21.2 %all-to-all-start.2 = ((f32[32,1,64]{2,1,0:T(1,128)}), f32[32,1,64]{2,1,0:T(1,128)S(1)}, u32[]{:S(2)}, u32[]{:S(2)}) async-start(f32[32,1,64]{2,1,0:T(1,128)} %broadcast_in_dim.31), calls=%async_computation.2 | async-start | bytes 32768 | tf_op jit(solution)/shard_map/all_to_all | solution.py:12
  169.5 17.0 %collective-permute-start.2 = (bf16[2,1,64,640]{3,2,0,1:T(8,128)(2,1)S(1)}, bf16[2,1,64,640]{3,2,0,1:T(8,128)(2,1)S(1)}, u32[]{:S(2)}, u32[]{:S(2)}) collective-permute-start(bf16[2,1,64,640]{3,2,0,1:T(8,128)(2,1)S(1)} %fusion.50), channel_id=1, source_target_pairs={{0,1},{1,2},{2,3},{3,4},{4,5},{5,6},{6,7},{7,8},{8,9},{9,10},{10,1... | collective-permute-start | bytes 491528 | tf_op jit(solution)/shard_map/ppermute | solution.py:34
  172.0 14.5 %collective-permute-start.3 = (bf16[2,1,64,640]{3,2,0,1:T(8,128)(2,1)S(1)}, bf16[2,1,64,640]{3,2,0,1:T(8,128)(2,1)S(1)}, u32[]{:S(2)}, u32[]{:S(2)}) collective-permute-start(bf16[2,1,64,640]{3,2,0,1:T(8,128)(2,1)S(1)} %fusion.50), channel_id=1, source_target_pairs={{1,0},{2,1},{3,2},{4,3},{5,4},{6,5},{7,6},{8,7},{9,8},{10,9},{11,1... | collective-permute-start | bytes 491528 | tf_op jit(solution)/shard_map/ppermute | solution.py:37
  205.0 1.8 copy-start.5
  205.0 1.8 copy-start.11
  205.0 1.8 copy-start.12
  206.8 24.3 %copy-start.1 = (bf16[9,40,20]{1,2,0:T(8,128)(2,1)S(1)}, bf16[9,40,20]{1,2,0:T(8,128)(2,1)}, u32[]{:S(2)}) copy-start(bf16[9,40,20]{1,2,0:T(8,128)(2,1)} %param.13) | copy-start | bytes 43204
Sparse Core Ops, SparseCore 0:
  52.5 50.3 all-gather.2
  105.0 52.5 all-gather.4
where the time goes:
time: 241 us; the launch traced here: 238 us
  local copies, waits for them, and re-layouts  108 us (45%)
  blocking collectives  64.3 us (27%)
  starting transfers between devices  25 us (10%)
  waiting for transfers between devices  14.6 us (6%)
  between operations  13.9 us (6%)
  matrix products  9.64 us (4%)
  other arithmetic  2.56 us (1%)
    all_to_all x3, blocking collectives, from_everyone(): lax.all_to_all(jnp.broadcast_to(shard[None], (length, *shard.shape)), axi...  64.3 us
    another operation x20, local copies, waits for them, and re-layouts, conv_backward(): stacked = jnp.stack(shifted, axis=1)  36.9 us
    transpose x2, local copies, waits for them, and re-layouts, conv_backward(): jnp.transpose(section, (0, 2, 1)).reshape(9 * channels, section.shape[1])  24.9 us
    reshape x4, local copies, waits for them, and re-layouts, joined_along(): tiles.reshape(*lengths[:dim], lengths[dim] * lengths[dim + 1], *lengths[d...  24.8 us
    all_to_all x2, starting transfers between devices, from_everyone(): lax.all_to_all(jnp.broadcast_to(shard[None], (length, *shard.shape)), axi...  16 us
    all_to_all x2, waiting for transfers between devices, from_everyone(): lax.all_to_all(jnp.broadcast_to(shard[None], (length, *shard.shape)), axi...  13.9 us
    unnamed x32, local copies, waits for them, and re-layouts  9.82 us
    dot_general x2, matrix products, conv_backward(): result = jnp.dot(flat_windows, flat, preferred_element_type=jnp.float32)  9.64 us
  transfers between devices with their start and end apart: 8, of which 3 were waited for; matrix products, arithmetic and copies ran while one was open for 31% of the time, Pallas kernels for 0%

commit v1 on v0

v1 whole, which is shorter than its diff:
```python
import jax
import jax.numpy as jnp
from jax import lax
from jax.experimental import pallas as pl
from jax.experimental.pallas import tpu as pltpu
from jax.sharding import PartitionSpec as P

MESH = pl.DeviceIdType.MESH
F32 = jnp.float32
BF16 = jnp.bfloat16
NX, NY, NZ = 4, 8, 8
CH = 640
BLK = 160
PX = 128
NUMBER = 32 * 64 * 40


def dev(x, y, z, c):
    return (2 * z + c, 4 * y + x)


def iota(shape, dim):
    return lax.broadcasted_iota(jnp.int32, shape, dim)


def dot(a, b, **kw):
    return jnp.dot(a, b, preferred_element_type=F32, **kw)


def group_of(lane):
    g = jnp.zeros_like(lane)
    for edge in (40, 80, 120, 160):
        g = g + (lane >= edge).astype(jnp.int32)
    return g


def kernel(
    wb, cot, hid, lat, par, out,
    W, RA, G, Gh, Hs, Hc, SS, ST, HBs, HBr, AC, BK, Os, Oc, CC,
    sA, sA0, rA, lsem, sR, rR, sP, rP, sG, rG, sGh, rGh, sH, rH, sS, rS, sB, rB, sO, rO,
):
    dp = lax.axis_index("dp")
    rr = lax.axis_index("rows")
    c = lax.rem(dp, 2)
    z = lax.div(dp, 2)
    x = lax.rem(rr, NX)
    y = lax.div(rr, NX)

    def remote(src, dst, ss, rs, target):
        return pltpu.make_async_remote_copy(
            src_ref=src, dst_ref=dst, send_sem=ss, recv_sem=rs, device_id=target,
            device_id_type=MESH,
        )

    def local_wait(ref, sem):
        pltpu.make_async_copy(ref, ref, sem).wait()

    X = lax.div(z, 2)
    slot = lax.rem(z, 2) * 4 + x
    for f in (1, 0):
        for k in range(8):
            if f == 1:
                z_, y_ = lax.rem(z + k, NZ), y
                mine = x == X
            else:
                z_, y_ = y, lax.rem(y + k, NY)
                mine = jnp.logical_and(x == X, y == z)
            target = dev(X, y_, z_, c)
            if k == 0:
                @pl.when(mine)
                def _():
                    pltpu.make_async_copy(wb.at[f], RA.at[f, slot], rA.at[f]).start()

                @pl.when(jnp.logical_not(mine))
                def _():
                    remote(wb.at[f], RA.at[f, slot], sA0.at[f], rA.at[f], target).start()
            else:
                remote(wb.at[f], RA.at[f, slot], sA.at[f], rA.at[f], target).start()

    for k in range(1, NX):
        t = lax.rem(x + k, NX)
        remote(cot, G.at[x], sG, rG, dev(t, y, z, c)).start()
    own_cot = pltpu.make_async_copy(cot, G.at[x], lsem)
    own_cot.start()

    for a, ref in enumerate((hid, lat)):
        v = ref[...].astype(F32)
        for k in range(NX):
            blk = v[:, BLK * k : BLK * k + BLK]
            blk = jnp.concatenate([blk, jnp.zeros((PX, 256 - BLK), F32)], axis=1)
            Hs[k, a] = blk.astype(BF16)
    for k in range(1, NX):
        t = lax.rem(x + k, NX)
        remote(Hs.at[t], Hc.at[x], sH, rH, dev(t, y, z, c)).start()
    Hc[x] = Hs[x]

    def region(f, cc, a, o):
        return W.at[f, cc, a, pl.ds(pl.multiple_of(80 * o, 16), 80), :]

    om = iota((80, 128), 0)
    mm_ = iota((80, 128), 1)
    hit = jnp.zeros((80, 128), jnp.bool_)
    for k in range(4):
        hit = jnp.logical_or(
            hit,
            jnp.logical_and(
                jnp.logical_and(mm_ >= 32 * k, mm_ < 32 * k + 20), om == mm_ - 12 * k
            ),
        )
    join = hit.astype(F32).astype(BF16)

    place = {1: y, 0: z}

    def at(f, p):
        return dev(x, p, z, c) if f == 1 else dev(x, y, p, c)

    def up(f, s, a):
        p = place[f]
        o = lax.rem(p - s + 8, 8)
        return remote(
            region(f, c, a, o), region(f, c, a, o), sR.at[f], rR.at[f, 0, s, a],
            at(f, lax.rem(p + 1, 8)),
        )

    def down(f, s, a):
        p = place[f]
        o = lax.rem(p + s, 8)
        return remote(
            region(f, c, a, o), region(f, c, a, o), sR.at[f], rR.at[f, 1, s, a],
            at(f, lax.rem(p + 7, 8)),
        )

    def share(f, a, o):
        o = lax.rem(o + 8, 8)
        remote(
            region(f, c, a, o), region(f, c, a, o), sP.at[f], rP.at[f], dev(x, y, z, 1 - c)
        ).start()

    for f in (1, 0):
        local_wait(RA.at[f], rA.at[f])
        for b in range(2):
            piece = dot(join, RA[f, 4 * b : 4 * b + 4].reshape(128, 384)).astype(BF16)
            for a in range(3):
                W[
                    f, c, a, pl.ds(pl.multiple_of(80 * place[f], 16), 80),
                    128 * b : 128 * b + 128,
                ] = piece[:, 128 * a : 128 * a + 128]
        for a in range(3):
            up(f, 0, a).start()
            down(f, 0, a).start()
            share(f, a, place[f])

    local_wait(Hc.at[0:3], rH)
    lane = iota((8, 256), 1)
    row8 = iota((8, 256), 0)
    sums = jnp.zeros((8, 256), F32)
    for a in range(2):
        for img in range(2):
            tot = jnp.zeros((1, 256), F32)
            sq = jnp.zeros((1, 256), F32)
            for t in range(NX):
                v = Hc[t, a, 64 * img : 64 * img + 64, :].astype(F32)
                tot = tot + jnp.sum(v, axis=0, keepdims=True)
                sq = sq + jnp.sum(v * v, axis=0, keepdims=True)
            sums = jnp.where(row8 == 4 * a + img, tot, sums)
            sums = jnp.where(row8 == 4 * a + 2 + img, sq, sums)

    def send_sums(p, value):
        SS[p] = value
        ST[p, y] = value
        for k in range(1, NY):
            remote(
                SS.at[p], ST.at[p, y], sS.at[p], rS.at[p], dev(x, lax.rem(y + k, NY), z, c)
            ).start()

    gi = group_of(iota((256, 256), 0))
    gj = group_of(iota((256, 256), 1))
    same = jnp.logical_and(gi == gj, gi < 4).astype(F32)

    def take_sums(p):
        local_wait(ST.at[p, 0:7], rS.at[p])
        tot = ST[p, 0]
        for k in range(1, NY):
            tot = tot + ST[p, k]
        return dot(tot, same, precision=lax.Precision.HIGHEST) / NUMBER

    send_sums(0, sums)

    for s in range(4):
        for f in (1, 0):
            for a in range(3):
                up(f, s, a).wait_recv()
                if s < 3:
                    up(f, s + 1, a).start()
                share(f, a, place[f] - 1 - s)
                if s < 3:
                    down(f, s, a).wait_recv()
                    if s < 2:
                        down(f, s + 1, a).start()
                    share(f, a, place[f] + 1 + s)

    mean = take_sums(0)
    stats = []
    for a in range(2):
        avg = mean[4 * a : 4 * a + 2]
        inv = lax.rsqrt(mean[4 * a + 2 : 4 * a + 4] - avg * avg + 1e-05)
        stats.append((avg, inv))

    own_cot.wait()
    local_wait(G.at[0:3], rG)
    pick = (iota((CH, 256), 0) == iota((CH, 256), 1) + BLK * x) & (iota((CH, 256), 1) < BLK)
    pick = pick.astype(F32).astype(BF16)
    for t in range(NX):
        CC[t] = dot(G[t], pick)

    def combine(accs):
        rows = accs[0].shape[0]
        q = jnp.bitwise_and(iota((rows, 128), 0), 63)
        ln = iota((rows, 128), 1)
        t0 = jnp.zeros((rows, 128), F32)
        t1 = jnp.zeros((rows, 128), F32)
        for j in range(4):
            b = j // 2
            blk = accs[j % 2][:, 128 * b : 128 * b + 128]
            low = jnp.where(q == 63, 0.0, pltpu.roll(blk, rows - 1, 0))
            mid = pltpu.roll(blk, 128 - 40, 1)
            high = jnp.where(q == 0, 0.0, pltpu.roll(pltpu.roll(blk, 128 - 80, 1), 1, 0))
            v = jnp.where(ln < 40, low + mid + high, 0.0)
            if j:
                v = pltpu.roll(v, 40 * j, 1)
            if j < 3:
                t0 = t0 + v
            else:
                t0 = t0 + jnp.where(ln >= 120, v, 0.0)
                t1 = jnp.where(ln < 32, v, 0.0)
        return jnp.concatenate([t0, t1], axis=1)

    def conv(n, f, mul):
        for e, (ai, t) in enumerate(((0, 0), (2, 3))):
            HBs[n, e] = combine([mul(f, cc, ai, t, t + 1) for cc in range(2)])

        @pl.when(y > 0)
        def _():
            remote(HBs.at[n, 0], HBr.at[n, 0], sB.at[n, 0], rB.at[n, 0], dev(x, lax.rem(y + 7, 8), z, c)).start()

        @pl.when(y < NY - 1)
        def _():
            remote(HBs.at[n, 1], HBr.at[n, 1], sB.at[n, 1], rB.at[n, 1], dev(x, lax.rem(y + 1, 8), z, c)).start()

        for cc in range(2):
            AC[cc] = mul(f, cc, 1, 0, 4)
            AC[cc, 0:384] += mul(f, cc, 0, 1, 4)
            AC[cc, 128:512] += mul(f, cc, 2, 0, 3)
        BK[...] = combine([AC[0], AC[1]])

        @pl.when(y < NY - 1)
        def _():
            local_wait(HBr.at[n, 0], rB.at[n, 0])
            BK[384:512] += HBr[n, 0]

        @pl.when(y > 0)
        def _():
            local_wait(HBr.at[n, 1], rB.at[n, 1])
            BK[0:128] += HBr[n, 1]

    def mul_cot(f, cc, ai, t0, t1):
        return dot(G[t0:t1].reshape((t1 - t0) * PX, CH), W[f, cc, ai])

    def mul_grad(f, cc, ai, t0, t1):
        acc = None
        for k in range(NX):
            v = dot(
                Gh[k, t0 * PX : t1 * PX, 0:BLK], W[f, cc, ai, BLK * k : BLK * k + BLK, :]
            )
            acc = v if acc is None else acc + v
        return acc

    def norm_sums(n, a, gain, shift):
        avg, inv = stats[a]
        first = [jnp.zeros((1, 256), F32)] * 2
        second = [jnp.zeros((1, 256), F32)] * 2
        for t in range(NX):
            for img in range(2):
                px = slice(t * PX + 64 * img, t * PX + 64 * img + 64)
                v = Hc[t, a, 64 * img : 64 * img + 64, :].astype(F32)
                normed = (v - avg[img : img + 1]) * inv[img : img + 1]
                linear = normed * gain + shift
                s = jax.nn.sigmoid(linear)
                scaled = BK[px, :] * s * (1.0 + linear * (1.0 - s)) * gain
                BK[px, :] = scaled
                first[img] = first[img] + jnp.sum(scaled, axis=0, keepdims=True)
                second[img] = second[img] + jnp.sum(scaled * normed, axis=0, keepdims=True)
        value = jnp.zeros((8, 256), F32)
        for img in range(2):
            value = jnp.where(row8 == img, first[img], value)
            value = jnp.where(row8 == 2 + img, second[img], value)
        send_sums(n, value)
        got = take_sums(n)
        return got[0:2], got[2:4]

    def norm_apply(a, t, img, first, second):
        avg, inv = stats[a]
        px = slice(t * PX + 64 * img, t * PX + 64 * img + 64)
        v = Hc[t, a, 64 * img : 64 * img + 64, :].astype(F32)
        i_ = inv[img : img + 1]
        normed = (v - avg[img : img + 1]) * i_
        return i_ * (BK[px, :] - first[img : img + 1] - normed * second[img : img + 1])

    par_x = par[x]
    local_wait(W.at[1, 1 - c], rP.at[1])
    conv(0, 1, mul_cot)
    first, second = norm_sums(1, 0, par_x[0:1], par_x[1:2])
    for t in range(NX):
        for img in range(2):
            px = slice(t * PX + 64 * img, t * PX + 64 * img + 64)
            Gh[x, px, :] = norm_apply(0, t, img, first, second).astype(BF16)
    for k in range(1, NX):
        remote(Gh.at[x], Gh.at[x], sGh, rGh, dev(lax.rem(x + k, NX), y, z, c)).start()
    local_wait(W.at[0, 1 - c], rP.at[0])
    local_wait(Gh.at[0:3], rGh)

    conv(1, 0, mul_grad)
    first, second = norm_sums(2, 1, par_x[2:3], par_x[3:4])
    for t in range(NX):
        for img in range(2):
            q = slice(64 * img, 64 * img + 64)
            v = CC[t, q, :] + norm_apply(1, t, img, first, second)
            Os[t, q, :] = v.astype(BF16)
    for k in range(1, NX):
        t = lax.rem(x + k, NX)
        remote(Os.at[t], Oc.at[x], sO, rO, dev(t, y, z, c)).start()
    Oc[x] = Os[x]

    for f in (1, 0):
        if f == 1:
            mine = x == X
        else:
            mine = jnp.logical_and(x == X, y == z)
        local_wait(RA.at[f, 0:7], sA.at[f])

        @pl.when(jnp.logical_not(mine))
        def _():
            local_wait(RA.at[f, 0], sA0.at[f])

        local_wait(W.at[f, 0, :, 0:560, :], sR.at[f])
        local_wait(W.at[f, 0], sP.at[f])
    local_wait(G.at[0:3], sG)
    local_wait(Gh.at[0:3], sGh)
    local_wait(Hc.at[0:3], sH)
    for p in range(3):
        local_wait(ST.at[p, 0:7], sS.at[p])
    for n in range(2):
        @pl.when(y > 0)
        def _():
            local_wait(HBs.at[n, 0], sB.at[n, 0])

        @pl.when(y < NY - 1)
        def _():
            local_wait(HBs.at[n, 1], sB.at[n, 1])

    local_wait(Oc.at[0:3], rO)
    local_wait(Oc.at[0:3], sO)
    out[...] = jnp.concatenate([Oc[k, :, 0:BLK].astype(F32) for k in range(NX)], axis=1).astype(
        BF16
    )


def body(latent, hidden, cotangent, filter_one, filter_two, gain_one, shift_one, gain_two, shift_two):
    both = jnp.stack([filter_one, filter_two]).reshape(2, 3, 120, 20)
    wb = jnp.transpose(both, (0, 3, 1, 2))
    wb = jnp.pad(wb, ((0, 0), (0, 12), (0, 0), (0, 8))).reshape(2, 32, 384)
    par = jnp.stack([gain_two, shift_two, gain_one, shift_one]).reshape(4, NX, BLK)
    par = jnp.pad(jnp.transpose(par, (1, 0, 2)), ((0, 0), (0, 4), (0, 256 - BLK)))
    rows = [a.reshape(PX, CH) for a in (cotangent, hidden, latent)]
    vmem = pl.BlockSpec(memory_space=pltpu.VMEM)
    dma = pltpu.SemaphoreType.DMA
    out = pl.pallas_call(
        kernel,
        out_shape=jax.ShapeDtypeStruct((PX, CH), BF16),
        in_specs=[vmem] * 5,
        out_specs=vmem,
        scratch_shapes=[
            pltpu.VMEM((2, 2, 3, CH, 256), BF16),
            pltpu.VMEM((2, 8, 32, 384), BF16),
            pltpu.VMEM((NX, PX, CH), BF16),
            pltpu.VMEM((NX, NX * PX, 256), BF16),
            pltpu.VMEM((NX, 2, PX, 256), BF16),
            pltpu.VMEM((NX, 2, PX, 256), BF16),
            pltpu.VMEM((3, 8, 256), F32),
            pltpu.VMEM((3, NY, 8, 256), F32),
            pltpu.VMEM((2, 2, PX, 256), F32),
            pltpu.VMEM((2, 2, PX, 256), F32),
            pltpu.VMEM((2, NX * PX, 256), F32),
            pltpu.VMEM((NX * PX, 256), F32),
            pltpu.VMEM((NX, PX, 256), BF16),
            pltpu.VMEM((NX, PX, 256), BF16),
            pltpu.VMEM((NX, PX, 256), F32),
            dma((2,)), dma((2,)), dma((2,)), dma,
            dma((2,)), dma((2, 2, 4, 3)),
            dma((2,)), dma((2,)),
            dma, dma, dma, dma, dma, dma,
            dma((3,)), dma((3,)),
            dma((2, 2)), dma((2, 2)),
            dma, dma,
        ],
        compiler_params=pltpu.CompilerParams(
            has_side_effects=True, vmem_limit_bytes=48 * 1024 * 1024
        ),
        name="block_backward",
    )(wb, *rows, par)
    return out.reshape(latent.shape)


def solution(mesh):
    in_specs = (
        P("dp", "rows", None, None),
        P("dp", "rows", None, None),
        P("dp", "rows", None, None),
        P(None, "dp", "rows"),
        P(None, "dp", "rows"),
        P(),
        P(),
        P(),
        P(),
    )
    out_specs = P("dp", "rows", None, None)
    return jax.shard_map(body, mesh=mesh, in_specs=in_specs, out_specs=out_specs, check_vma=False)
```

time: 241 us -> 102 us (0.42)
  the two profiles are of different devices: /device:TPU:192 before, /device:TPU:8 now
where the time goes in v1:
time: 102 us
  Pallas kernels  96.8 us (95%)
  local copies, waits for them, and re-layouts  4.67 us (5%)
    pallas_call x1, Pallas kernels, body(): pl.pallas_call(kernel, out_shape=jax.ShapeDtypeStruct((PX, CH), BF16), in...  96.8 us
    unnamed x21, local copies, waits for them, and re-layouts  4.04 us

profile of v1, /device:TPU:8, one launch (start us, length us, event | category | flops | bytes accessed | tf_op | source)
XLA Modules:
  0.0 101.6 jit_solution(4645025305986041199)
XLA Ops:
  0.0 0.0 copy-start.5
  0.0 0.7 copy-done.5
  0.7 0.0 copy-start.6
  0.7 0.0 copy-start.7
  0.7 0.0 copy-start.8
  0.7 0.1 stack.29
  0.8 0.6 copy-done.6
  1.4 0.0 copy-start.3
  1.4 0.1 stack.30
  1.5 0.0 copy-done.7
  1.5 0.1 stack.27
  1.5 0.0 copy-done.8
  1.5 0.1 stack.28
  1.7 0.5 copy-done.3
  2.2 0.0 copy-start.4
  2.2 0.1 stack.24
  2.3 0.7 copy-done.4
  3.0 0.0 copy-start.2
  3.0 0.0 copy-start.1
  3.1 0.1 stack.25
  3.2 0.0 copy-start
  3.3 0.1 reshape.29.wb
  3.3 0.6 copy-done.2
  3.9 0.1 copy-done.1
  4.0 0.1 copy-done
  4.1 96.8 %block_backward.1 = bf16[128,640]{1,0:T(8,128)(2,1)S(1)} custom-call(bf16[2,32,384]{2,1,0:T(8,128)(2,1)S(1)} %reshape.29.wb, bf16[128,640]{1,0:T(8,128)(2,1)S(1)} %bitcast.15, bf16[128,640]{1,0:T(8,128)(2,1)S(1)} %bitcast.16, bf16[128,640]{1,0:T(8,128)(2,1)S(1)} %bitcast.17, f32[4,8,256]{2,1,0:T(8,128)S(1)} %pad.9.par), custom_call_target="tpu_custom_call" | custom-call | tf_op jit(solution)/shard_map/block_backward/pallas_call | solution.py:377
  101.0 0.7 copy.15
  (6 shorter events, 0.1 us)
Async XLA Ops:
  0.0 0.7 copy-start.5
  0.7 0.7 copy-start.6
  0.7 0.8 copy-start.7
  0.7 0.9 copy-start.8
  1.4 0.8 copy-start.3
  2.2 0.8 copy-start.4
  3.0 0.9 copy-start.2
  3.0 1.0 copy-start.1
  3.2 1.0 copy-start

commit v2 on v1

--- a/solution.py
+++ b/solution.py
@@ -35,9 +35,9 @@
 
 
 def kernel(
-    wb, cot, hid, lat, par, out,
-    W, RA, G, Gh, Hs, Hc, SS, ST, HBs, HBr, AC, BK, Os, Oc, CC,
-    sA, sA0, rA, lsem, sR, rR, sP, rP, sG, rG, sGh, rGh, sH, rH, sS, rS, sB, rB, sO, rO,
+    f1, f2, cot, hid, lat, g2, s2, g1, s1, out,
+    FV, PV, HV, WB, W, W1, RA, G, Gh, L, Hs, Hc, Hx, SS, ST, HBs, HBr, AC, BK, Os, Oc, CC,
+    lF, lP, lH, lC, sA, sA0, rA, sR, rR, sP, rP, sG, rG, sGh, rGh, sH, rH, sS, rS, sB, rB, sO, rO,
 ):
     dp = lax.axis_index("dp")
     rr = lax.axis_index("rows")
@@ -45,6 +45,9 @@
     z = lax.div(dp, 2)
     x = lax.rem(rr, NX)
     y = lax.div(rr, NX)
+    X = lax.div(z, 2)
+    mine_y = x == X
+    mine_z = jnp.logical_and(x == X, y == z)
 
     def remote(src, dst, ss, rs, target):
         return pltpu.make_async_remote_copy(
@@ -55,44 +58,91 @@
     def local_wait(ref, sem):
         pltpu.make_async_copy(ref, ref, sem).wait()
 
-    X = lax.div(z, 2)
+    bar = pltpu.get_barrier_semaphore()
+
+    def here(target):
+        pl.semaphore_signal(bar, inc=1, device_id=target, device_id_type=MESH)
+
+    for b in range(2):
+        zs = 2 * x + lax.rem(z + b, 2)
+        for k in range(NX):
+            xs = lax.rem(x + k, NX)
+            if b == 0 and k == 0:
+                @pl.when(jnp.logical_not(mine_y))
+                def _():
+                    here(dev(xs, y, zs, c))
+
+                @pl.when(jnp.logical_not(mine_z))
+                def _():
+                    here(dev(xs, z, zs, c))
+            else:
+                here(dev(xs, y, zs, c))
+                here(dev(xs, z, zs, c))
+    for k in range(1, NX):
+        here(dev(lax.rem(x + k, NX), y, z, c))
+    for k in range(1, NY):
+        here(dev(x, lax.rem(y + k, NY), z, c))
+    for k in (1, NZ - 1):
+        here(dev(x, y, lax.rem(z + k, NZ), c))
+    here(dev(x, y, z, 1 - c))
+
+    loads = [pltpu.make_async_copy(r, FV.at[f], lF.at[f]) for f, r in enumerate((f1, f2))]
+    loads += [pltpu.make_async_copy(r, HV.at[a], lH.at[a]) for a, r in enumerate((hid, lat))]
+    loads += [
+        pltpu.make_async_copy(r, PV[a], lP.at[a]) for a, r in enumerate((g2, s2, g1, s1))
+    ]
+    own_cot = pltpu.make_async_copy(cot, G.at[x], lC)
+    for load in loads[1::-1] + loads[2:]:
+        load.start()
+    own_cot.start()
+    WB[...] = jnp.zeros_like(WB)
+    for f in (1, 0):
+        loads[f].wait()
+        for a in range(3):
+            taps = [FV[f, 3 * a + b].astype(F32) for b in range(3)]
+            WB[f, 0:20, 128 * a : 128 * a + 128] = jnp.concatenate(
+                taps + [jnp.zeros((20, 8), F32)], axis=1
+            ).astype(BF16)
+    for a in range(2):
+        loads[2 + a].wait()
+    v = [HV[a].astype(F32) for a in range(2)]
+    for k in range(NX):
+        Hs[k] = jnp.concatenate(
+            [v[a][:, BLK * k : BLK * k + BLK] for a in range(2)] + [jnp.zeros((PX, 64), F32)],
+            axis=1,
+        ).astype(BF16)
+    params = []
+    for a in range(4):
+        loads[4 + a].wait()
+        whole = PV[a][...].reshape(1, CH)
+        p = jnp.zeros((1, BLK), F32)
+        for k in range(NX):
+            p = jnp.where(x == k, whole[:, BLK * k : BLK * k + BLK], p)
+        params.append(jnp.concatenate([p, jnp.zeros((1, 256 - BLK), F32)], axis=1))
+    own_cot.wait()
+
+    pl.semaphore_wait(
+        bar, 29 - mine_y.astype(jnp.int32) - mine_z.astype(jnp.int32)
+    )
+
     slot = lax.rem(z, 2) * 4 + x
     for f in (1, 0):
         for k in range(8):
             if f == 1:
-                z_, y_ = lax.rem(z + k, NZ), y
-                mine = x == X
+                z_, y_, mine = lax.rem(z + k, NZ), y, mine_y
             else:
-                z_, y_ = y, lax.rem(y + k, NY)
-                mine = jnp.logical_and(x == X, y == z)
+                z_, y_, mine = y, lax.rem(y + k, NY), mine_z
             target = dev(X, y_, z_, c)
             if k == 0:
                 @pl.when(mine)
                 def _():
-                    pltpu.make_async_copy(wb.at[f], RA.at[f, slot], rA.at[f]).start()
+                    pltpu.make_async_copy(WB.at[f], RA.at[f, slot], rA.at[f]).start()
 
                 @pl.when(jnp.logical_not(mine))
                 def _():
-                    remote(wb.at[f], RA.at[f, slot], sA0.at[f], rA.at[f], target).start()
+                    remote(WB.at[f], RA.at[f, slot], sA0.at[f], rA.at[f], target).start()
             else:
-                remote(wb.at[f], RA.at[f, slot], sA.at[f], rA.at[f], target).start()
-
-    for k in range(1, NX):
-        t = lax.rem(x + k, NX)
-        remote(cot, G.at[x], sG, rG, dev(t, y, z, c)).start()
-    own_cot = pltpu.make_async_copy(cot, G.at[x], lsem)
-    own_cot.start()
-
-    for a, ref in enumerate((hid, lat)):
-        v = ref[...].astype(F32)
-        for k in range(NX):
-            blk = v[:, BLK * k : BLK * k + BLK]
-            blk = jnp.concatenate([blk, jnp.zeros((PX, 256 - BLK), F32)], axis=1)
-            Hs[k, a] = blk.astype(BF16)
-    for k in range(1, NX):
-        t = lax.rem(x + k, NX)
-        remote(Hs.at[t], Hc.at[x], sH, rH, dev(t, y, z, c)).start()
-    Hc[x] = Hs[x]
+                remote(WB.at[f], RA.at[f, slot], sA.at[f], rA.at[f], target).start()
 
     def region(f, cc, a, o):
         return W.at[f, cc, a, pl.ds(pl.multiple_of(80 * o, 16), 80), :]
@@ -149,42 +199,14 @@
             up(f, 0, a).start()
             down(f, 0, a).start()
             share(f, a, place[f])
-
-    local_wait(Hc.at[0:3], rH)
-    lane = iota((8, 256), 1)
-    row8 = iota((8, 256), 0)
-    sums = jnp.zeros((8, 256), F32)
-    for a in range(2):
-        for img in range(2):
-            tot = jnp.zeros((1, 256), F32)
-            sq = jnp.zeros((1, 256), F32)
-            for t in range(NX):
-                v = Hc[t, a, 64 * img : 64 * img + 64, :].astype(F32)
-                tot = tot + jnp.sum(v, axis=0, keepdims=True)
-                sq = sq + jnp.sum(v * v, axis=0, keepdims=True)
-            sums = jnp.where(row8 == 4 * a + img, tot, sums)
-            sums = jnp.where(row8 == 4 * a + 2 + img, sq, sums)
-
-    def send_sums(p, value):
-        SS[p] = value
-        ST[p, y] = value
-        for k in range(1, NY):
-            remote(
-                SS.at[p], ST.at[p, y], sS.at[p], rS.at[p], dev(x, lax.rem(y + k, NY), z, c)
-            ).start()
-
-    gi = group_of(iota((256, 256), 0))
-    gj = group_of(iota((256, 256), 1))
-    same = jnp.logical_and(gi == gj, gi < 4).astype(F32)
-
-    def take_sums(p):
-        local_wait(ST.at[p, 0:7], rS.at[p])
-        tot = ST[p, 0]
-        for k in range(1, NY):
-            tot = tot + ST[p, k]
-        return dot(tot, same, precision=lax.Precision.HIGHEST) / NUMBER
-
-    send_sums(0, sums)
+        if f == 1:
+            for k in range(1, NX):
+                t = lax.rem(x + k, NX)
+                remote(G.at[x], G.at[x], sG, rG, dev(t, y, z, c)).start()
+            for k in range(1, NX):
+                t = lax.rem(x + k, NX)
+                remote(Hs.at[t], Hc.at[x], sH, rH, dev(t, y, z, c)).start()
+            Hc[x] = Hs[x]
 
     for s in range(4):
         for f in (1, 0):
@@ -199,19 +221,44 @@
                         down(f, s + 1, a).start()
                     share(f, a, place[f] + 1 + s)
 
-    mean = take_sums(0)
-    stats = []
-    for a in range(2):
-        avg = mean[4 * a : 4 * a + 2]
-        inv = lax.rsqrt(mean[4 * a + 2 : 4 * a + 4] - avg * avg + 1e-05)
-        stats.append((avg, inv))
-
-    own_cot.wait()
-    local_wait(G.at[0:3], rG)
-    pick = (iota((CH, 256), 0) == iota((CH, 256), 1) + BLK * x) & (iota((CH, 256), 1) < BLK)
-    pick = pick.astype(F32).astype(BF16)
-    for t in range(NX):
-        CC[t] = dot(G[t], pick)
+    row8 = iota((8, 256), 0)
+    local_wait(Hc.at[0:3], rH)
+    zero = jnp.zeros((64, 256 - BLK), F32)
+    sums = jnp.zeros((8, 256), F32)
+    for img in range(2):
+        tot = [jnp.zeros((1, 256), F32)] * 2
+        sq = [jnp.zeros((1, 256), F32)] * 2
+        for t in range(NX):
+            both = Hc[t, 64 * img : 64 * img + 64, :].astype(F32)
+            for a in range(2):
+                v = jnp.concatenate([both[:, BLK * a : BLK * a + BLK], zero], axis=1)
+                Hx[a, t, 64 * img : 64 * img + 64, :] = v
+                tot[a] = tot[a] + jnp.sum(v, axis=0, keepdims=True)
+                sq[a] = sq[a] + jnp.sum(v * v, axis=0, keepdims=True)
+        for a in range(2):
+            sums = jnp.where(row8 == 4 * a + img, tot[a], sums)
+            sums = jnp.where(row8 == 4 * a + 2 + img, sq[a], sums)
+
+    def send_sums(p, value):
+        SS[p] = value
+        ST[p, y] = value
+        for k in range(1, NY):
+            remote(
+                SS.at[p], ST.at[p, y], sS.at[p], rS.at[p], dev(x, lax.rem(y + k, NY), z, c)
+            ).start()
+
+    gi = group_of(iota((256, 256), 0))
+    gj = group_of(iota((256, 256), 1))
+    same = jnp.logical_and(gi == gj, gi < 4).astype(F32)
+
+    def take_sums(p):
+        local_wait(ST.at[p, 0:7], rS.at[p])
+        tot = ST[p, 0]
+        for k in range(1, NY):
+            tot = tot + ST[p, k]
+        return dot(tot, same, precision=lax.Precision.HIGHEST) / NUMBER
+
+    send_sums(0, sums)
 
     def combine(accs):
         rows = accs[0].shape[0]
@@ -267,13 +314,7 @@
         return dot(G[t0:t1].reshape((t1 - t0) * PX, CH), W[f, cc, ai])
 
     def mul_grad(f, cc, ai, t0, t1):
-        acc = None
-        for k in range(NX):
-            v = dot(
-                Gh[k, t0 * PX : t1 * PX, 0:BLK], W[f, cc, ai, BLK * k : BLK * k + BLK, :]
-            )
-            acc = v if acc is None else acc + v
-        return acc
+        return dot(L[t0 * PX : t1 * PX, :], W1[cc, ai])
 
     def norm_sums(n, a, gain, shift):
         avg, inv = stats[a]
@@ -282,7 +323,7 @@
         for t in range(NX):
             for img in range(2):
                 px = slice(t * PX + 64 * img, t * PX + 64 * img + 64)
-                v = Hc[t, a, 64 * img : 64 * img + 64, :].astype(F32)
+                v = Hx[a, t, 64 * img : 64 * img + 64, :]
                 normed = (v - avg[img : img + 1]) * inv[img : img + 1]
                 linear = normed * gain + shift
                 s = jax.nn.sigmoid(linear)
@@ -295,32 +336,62 @@
             value = jnp.where(row8 == img, first[img], value)
             value = jnp.where(row8 == 2 + img, second[img], value)
         send_sums(n, value)
+        if n == 1:
+            spare_time()
         got = take_sums(n)
         return got[0:2], got[2:4]
 
     def norm_apply(a, t, img, first, second):
         avg, inv = stats[a]
         px = slice(t * PX + 64 * img, t * PX + 64 * img + 64)
-        v = Hc[t, a, 64 * img : 64 * img + 64, :].astype(F32)
+        v = Hx[a, t, 64 * img : 64 * img + 64, :]
         i_ = inv[img : img + 1]
         normed = (v - avg[img : img + 1]) * i_
         return i_ * (BK[px, :] - first[img : img + 1] - normed * second[img : img + 1])
 
-    par_x = par[x]
+    def spare_time():
+        pick = (iota((CH, 256), 0) == iota((CH, 256), 1) + BLK * x) & (iota((CH, 256), 1) < BLK)
+        pick = pick.astype(F32).astype(BF16)
+        for t in range(NX):
+            CC[t] = dot(G[t], pick)
+        local_wait(W.at[0, 1 - c], rP.at[0])
+        for k in range(NX):
+            W1[:, :, 128 * k : 128 * k + 128, :] = W[0, :, :, BLK * k : BLK * k + 128, :]
+            W1[:, :, 512 + 32 * k : 544 + 32 * k, :] = W[0, :, :, BLK * k + 128 : BLK * k + BLK, :]
+
+    local_wait(G.at[0:3], rG)
     local_wait(W.at[1, 1 - c], rP.at[1])
     conv(0, 1, mul_cot)
-    first, second = norm_sums(1, 0, par_x[0:1], par_x[1:2])
-    for t in range(NX):
-        for img in range(2):
-            px = slice(t * PX + 64 * img, t * PX + 64 * img + 64)
-            Gh[x, px, :] = norm_apply(0, t, img, first, second).astype(BF16)
+    mean = take_sums(0)
+    stats = []
+    for a in range(2):
+        avg = mean[4 * a : 4 * a + 2]
+        inv = lax.rsqrt(mean[4 * a + 2 : 4 * a + 4] - avg * avg + 1e-05)
+        stats.append((avg, inv))
+    first, second = norm_sums(1, 0, params[0], params[1])
+    for img in range(2):
+        rest = jnp.zeros((64, 128), F32)
+        for t in range(NX):
+            v = norm_apply(0, t, img, first, second)
+            Gh[x, t * PX + 64 * img : t * PX + 64 * img + 64, :] = v[:, 0:128].astype(BF16)
+            rest = rest + (pltpu.roll(v[:, 128:256], 32 * t, 1) if t else v[:, 128:256])
+        Gh[x, 512 + 64 * img : 576 + 64 * img, :] = rest.astype(BF16)
     for k in range(1, NX):
         remote(Gh.at[x], Gh.at[x], sGh, rGh, dev(lax.rem(x + k, NX), y, z, c)).start()
-    local_wait(W.at[0, 1 - c], rP.at[0])
     local_wait(Gh.at[0:3], rGh)
+    lane = iota((PX, 128), 1)
+    rests = [Gh[k, 512:640, :].astype(F32) for k in range(NX)]
+    for k in range(NX):
+        L[:, 128 * k : 128 * k + 128] = Gh[k, 0:512, :]
+    for t in range(NX):
+        v = jnp.zeros((PX, 128), F32)
+        for k in range(NX):
+            w = pltpu.roll(rests[k], (32 * (k - t)) % 128, 1) if k != t else rests[k]
+            v = jnp.where((lane >= 32 * k) & (lane < 32 * k + 32), w, v)
+        L[t * PX : t * PX + PX, 512:640] = v.astype(BF16)
 
     conv(1, 0, mul_grad)
-    first, second = norm_sums(2, 1, par_x[2:3], par_x[3:4])
+    first, second = norm_sums(2, 1, params[2], params[3])
     for t in range(NX):
         for img in range(2):
             q = slice(64 * img, 64 * img + 64)
@@ -332,10 +403,7 @@
     Oc[x] = Os[x]
 
     for f in (1, 0):
-        if f == 1:
-            mine = x == X
-        else:
-            mine = jnp.logical_and(x == X, y == z)
+        mine = mine_y if f == 1 else mine_z
         local_wait(RA.at[f, 0:7], sA.at[f])
 
         @pl.when(jnp.logical_not(mine))
@@ -366,26 +434,31 @@
 
 
 def body(latent, hidden, cotangent, filter_one, filter_two, gain_one, shift_one, gain_two, shift_two):
-    both = jnp.stack([filter_one, filter_two]).reshape(2, 3, 120, 20)
-    wb = jnp.transpose(both, (0, 3, 1, 2))
-    wb = jnp.pad(wb, ((0, 0), (0, 12), (0, 0), (0, 8))).reshape(2, 32, 384)
-    par = jnp.stack([gain_two, shift_two, gain_one, shift_one]).reshape(4, NX, BLK)
-    par = jnp.pad(jnp.transpose(par, (1, 0, 2)), ((0, 0), (0, 4), (0, 256 - BLK)))
+    filters = [jnp.transpose(a, (0, 2, 1)) for a in (filter_one, filter_two)]
     rows = [a.reshape(PX, CH) for a in (cotangent, hidden, latent)]
+    params = (gain_two, shift_two, gain_one, shift_one)
     vmem = pl.BlockSpec(memory_space=pltpu.VMEM)
+    anywhere = pl.BlockSpec(memory_space=pl.ANY)
     dma = pltpu.SemaphoreType.DMA
     out = pl.pallas_call(
         kernel,
         out_shape=jax.ShapeDtypeStruct((PX, CH), BF16),
-        in_specs=[vmem] * 5,
+        in_specs=[anywhere] * 9,
         out_specs=vmem,
         scratch_shapes=[
+            pltpu.VMEM((2, 9, 20, 40), BF16),
+            [pltpu.VMEM((CH,), F32)] * 4,
+            pltpu.VMEM((2, PX, CH), BF16),
+            pltpu.VMEM((2, 32, 384), BF16),
             pltpu.VMEM((2, 2, 3, CH, 256), BF16),
+            pltpu.VMEM((2, 3, CH, 256), BF16),
             pltpu.VMEM((2, 8, 32, 384), BF16),
             pltpu.VMEM((NX, PX, CH), BF16),
-            pltpu.VMEM((NX, NX * PX, 256), BF16),
-            pltpu.VMEM((NX, 2, PX, 256), BF16),
-            pltpu.VMEM((NX, 2, PX, 256), BF16),
+            pltpu.VMEM((NX, 640, 128), BF16),
+            pltpu.VMEM((NX * PX, CH), BF16),
+            pltpu.VMEM((NX, PX, 384), BF16),
+            pltpu.VMEM((NX, PX, 384), BF16),
+            pltpu.VMEM((2, NX, PX, 256), F32),
             pltpu.VMEM((3, 8, 256), F32),
             pltpu.VMEM((3, NY, 8, 256), F32),
             pltpu.VMEM((2, 2, PX, 256), F32),
@@ -395,7 +468,8 @@
             pltpu.VMEM((NX, PX, 256), BF16),
             pltpu.VMEM((NX, PX, 256), BF16),
             pltpu.VMEM((NX, PX, 256), F32),
-            dma((2,)), dma((2,)), dma((2,)), dma,
+            dma((2,)), dma((4,)), dma((2,)), dma,
+            dma((2,)), dma((2,)), dma((2,)),
             dma((2,)), dma((2, 2, 4, 3)),
             dma((2,)), dma((2,)),
             dma, dma, dma, dma, dma, dma,
@@ -404,10 +478,10 @@
             dma, dma,
         ],
         compiler_params=pltpu.CompilerParams(
-            has_side_effects=True, vmem_limit_bytes=48 * 1024 * 1024
+            collective_id=0, has_side_effects=True, vmem_limit_bytes=62 * 1024 * 1024
         ),
         name="block_backward",
-    )(wb, *rows, par)
+    )(*filters, *rows, *params)
     return out.reshape(latent.shape)
 
 

time: 102 us -> 82.7 us (0.81)
  Pallas kernels: 96.8 us -> 80.9 us
  local copies, waits for them, and re-layouts: 4.67 us -> 1.6 us
    pallas_call x1, Pallas kernels: 96.8 us -> 80.9 us  [body(): pl.pallas_call(kernel, out_shape=jax.ShapeDtypeStruct((PX, CH), BF16), in...]
    unnamed x21 -> x1, local copies, waits for them, and re-layouts: 4.04 us -> 1.6 us
where the time goes in v2:
time: 82.7 us; the launch traced here: 82.5 us
  Pallas kernels  80.9 us (98%)
  local copies, waits for them, and re-layouts  1.6 us (2%)
    pallas_call x1, Pallas kernels, body(): pl.pallas_call(kernel, out_shape=jax.ShapeDtypeStruct((PX, CH), BF16), in...  80.9 us

profile of v2, /device:TPU:8, one launch (start us, length us, event | category | flops | bytes accessed | tf_op | source)
XLA Modules:
  0.0 82.5 jit_solution(18375363559266692805)
XLA Ops:
  0.0 80.9 %block_backward.1 = bf16[128,640]{1,0:T(8,128)(2,1)} custom-call(bf16[9,20,40]{2,1,0:T(8,128)(2,1)} %bitcast.12, bf16[9,20,40]{2,1,0:T(8,128)(2,1)} %bitcast.13, bf16[128,640]{1,0:T(8,128)(2,1)} %bitcast.9, bf16[128,640]{1,0:T(8,128)(2,1)} %bitcast.10, bf16[128,640]{1,0:T(8,128)(2,1)} %bitcast.11, f32[640]{0:T(1024)} %g2.1, f32[640]{0:T(1024)} %s2_.1, ...), custom_call_target="tpu_custom_call" | custom-call | tf_op jit(solution)/shard_map/block_backward/pallas_call | solution.py:443
  80.9 1.6 %copy.12 = bf16[2,1,64,640]{3,2,1,0:T(8,128)(2,1)} copy(bf16[2,1,64,640]{3,2,1,0:T(8,128)(2,1)} %bitcast.8) | data formatting | bytes 327680

commit v3 on v2

--- a/solution.py
+++ b/solution.py
@@ -126,43 +126,52 @@
     )
 
     slot = lax.rem(z, 2) * 4 + x
-    for f in (1, 0):
+    along_y = {f: lax.rem(f + c, 2) == 1 for f in (1, 0)}
+    mine = {f: jnp.where(along_y[f], mine_y.astype(jnp.int32), mine_z.astype(jnp.int32)) == 1 for f in (1, 0)}
+    place = {f: jnp.where(along_y[f], y, z) for f in (1, 0)}
+
+    def first_stage(f):
         for k in range(8):
-            if f == 1:
-                z_, y_, mine = lax.rem(z + k, NZ), y, mine_y
-            else:
-                z_, y_, mine = y, lax.rem(y + k, NY), mine_z
+            y_ = jnp.where(along_y[f], y, lax.rem(y + k, NY))
+            z_ = jnp.where(along_y[f], lax.rem(z + k, NZ), y)
             target = dev(X, y_, z_, c)
             if k == 0:
-                @pl.when(mine)
+                @pl.when(mine[f])
                 def _():
                     pltpu.make_async_copy(WB.at[f], RA.at[f, slot], rA.at[f]).start()
 
-                @pl.when(jnp.logical_not(mine))
+                @pl.when(jnp.logical_not(mine[f]))
                 def _():
                     remote(WB.at[f], RA.at[f, slot], sA0.at[f], rA.at[f], target).start()
             else:
                 remote(WB.at[f], RA.at[f, slot], sA.at[f], rA.at[f], target).start()
 
+    first_stage(1)
+    for k in range(1, NX):
+        t = lax.rem(x + k, NX)
+        remote(G.at[x], G.at[x], sG, rG, dev(t, y, z, c)).start()
+    for k in range(1, NX):
+        t = lax.rem(x + k, NX)
+        remote(Hs.at[t], Hc.at[x], sH, rH, dev(t, y, z, c)).start()
+    Hc[x] = Hs[x]
+
     def region(f, cc, a, o):
         return W.at[f, cc, a, pl.ds(pl.multiple_of(80 * o, 16), 80), :]
 
-    om = iota((80, 128), 0)
-    mm_ = iota((80, 128), 1)
-    hit = jnp.zeros((80, 128), jnp.bool_)
+    om = iota((80, 96), 0)
+    mm_ = iota((80, 96), 1)
+    hit = jnp.zeros((80, 96), jnp.bool_)
     for k in range(4):
         hit = jnp.logical_or(
             hit,
             jnp.logical_and(
-                jnp.logical_and(mm_ >= 32 * k, mm_ < 32 * k + 20), om == mm_ - 12 * k
+                jnp.logical_and(mm_ >= 24 * k, mm_ < 24 * k + 20), om == mm_ - 4 * k
             ),
         )
     join = hit.astype(F32).astype(BF16)
 
-    place = {1: y, 0: z}
-
     def at(f, p):
-        return dev(x, p, z, c) if f == 1 else dev(x, y, p, c)
+        return dev(x, jnp.where(along_y[f], p, y), jnp.where(along_y[f], z, p), c)
 
     def up(f, s, a):
         p = place[f]
@@ -186,10 +195,10 @@
             region(f, c, a, o), region(f, c, a, o), sP.at[f], rP.at[f], dev(x, y, z, 1 - c)
         ).start()
 
-    for f in (1, 0):
+    def start_ring(f):
         local_wait(RA.at[f], rA.at[f])
         for b in range(2):
-            piece = dot(join, RA[f, 4 * b : 4 * b + 4].reshape(128, 384)).astype(BF16)
+            piece = dot(join, RA[f, 4 * b : 4 * b + 4].reshape(96, 384)).astype(BF16)
             for a in range(3):
                 W[
                     f, c, a, pl.ds(pl.multiple_of(80 * place[f], 16), 80),
@@ -199,27 +208,23 @@
             up(f, 0, a).start()
             down(f, 0, a).start()
             share(f, a, place[f])
-        if f == 1:
-            for k in range(1, NX):
-                t = lax.rem(x + k, NX)
-                remote(G.at[x], G.at[x], sG, rG, dev(t, y, z, c)).start()
-            for k in range(1, NX):
-                t = lax.rem(x + k, NX)
-                remote(Hs.at[t], Hc.at[x], sH, rH, dev(t, y, z, c)).start()
-            Hc[x] = Hs[x]
-
+
+    def ring_step(f, s):
+        for a in range(3):
+            up(f, s, a).wait_recv()
+            if s < 3:
+                up(f, s + 1, a).start()
+            share(f, a, place[f] - 1 - s)
+            if s < 3:
+                down(f, s, a).wait_recv()
+                if s < 2:
+                    down(f, s + 1, a).start()
+                share(f, a, place[f] + 1 + s)
+
+    start_ring(1)
+    first_stage(0)
     for s in range(4):
-        for f in (1, 0):
-            for a in range(3):
-                up(f, s, a).wait_recv()
-                if s < 3:
-                    up(f, s + 1, a).start()
-                share(f, a, place[f] - 1 - s)
-                if s < 3:
-                    down(f, s, a).wait_recv()
-                    if s < 2:
-                        down(f, s + 1, a).start()
-                    share(f, a, place[f] + 1 + s)
+        ring_step(1, s)
 
     row8 = iota((8, 256), 0)
     local_wait(Hc.at[0:3], rH)
@@ -259,6 +264,22 @@
         return dot(tot, same, precision=lax.Precision.HIGHEST) / NUMBER
 
     send_sums(0, sums)
+    start_ring(0)
+
+    ln128 = iota((32, 128), 1)
+
+    def pack(v):
+        fold = v[0:32, 128:256]
+        for g in range(1, 4):
+            fold = fold + pltpu.roll(v[32 * g : 32 * g + 32, 128:256], 32 * g, 1)
+        return jnp.concatenate([v[:, 0:128], fold], axis=0)
+
+    def unpack(m):
+        fold = m[128:160]
+        rest = [jnp.where(ln128 < 32, fold, 0.0)]
+        for g in range(1, 4):
+            rest.append(jnp.where(ln128 < 32, pltpu.roll(fold, 128 - 32 * g, 1), 0.0))
+        return jnp.concatenate([m[0:128], jnp.concatenate(rest, axis=0)], axis=1)
 
     def combine(accs):
         rows = accs[0].shape[0]
@@ -284,7 +305,7 @@
 
     def conv(n, f, mul):
         for e, (ai, t) in enumerate(((0, 0), (2, 3))):
-            HBs[n, e] = combine([mul(f, cc, ai, t, t + 1) for cc in range(2)])
+            HBs[n, e] = pack(combine([mul(f, cc, ai, t, t + 1) for cc in range(2)]))
 
         @pl.when(y > 0)
         def _():
@@ -300,15 +321,12 @@
             AC[cc, 128:512] += mul(f, cc, 2, 0, 3)
         BK[...] = combine([AC[0], AC[1]])
 
-        @pl.when(y < NY - 1)
+    def take_halo(n, e):
+        @pl.when(y < NY - 1 if e == 0 else y > 0)
         def _():
-            local_wait(HBr.at[n, 0], rB.at[n, 0])
-            BK[384:512] += HBr[n, 0]
-
-        @pl.when(y > 0)
-        def _():
-            local_wait(HBr.at[n, 1], rB.at[n, 1])
-            BK[0:128] += HBr[n, 1]
+            local_wait(HBr.at[n, e], rB.at[n, e])
+            px = slice(384, 512) if e == 0 else slice(0, 128)
+            BK[px] += unpack(HBr[n, e])
 
     def mul_cot(f, cc, ai, t0, t1):
         return dot(G[t0:t1].reshape((t1 - t0) * PX, CH), W[f, cc, ai])
@@ -320,7 +338,11 @@
         avg, inv = stats[a]
         first = [jnp.zeros((1, 256), F32)] * 2
         second = [jnp.zeros((1, 256), F32)] * 2
-        for t in range(NX):
+        for t in (1, 2, 0, 3):
+            if t == 0:
+                take_halo(n - 1, 1)
+            if t == 3:
+                take_halo(n - 1, 0)
             for img in range(2):
                 px = slice(t * PX + 64 * img, t * PX + 64 * img + 64)
                 v = Hx[a, t, 64 * img : 64 * img + 64, :]
@@ -337,7 +359,9 @@
             value = jnp.where(row8 == 2 + img, second[img], value)
         send_sums(n, value)
         if n == 1:
+            ring_step(0, 1)
             spare_time()
+            ring_step(0, 2)
         got = take_sums(n)
         return got[0:2], got[2:4]
 
@@ -354,14 +378,11 @@
         pick = pick.astype(F32).astype(BF16)
         for t in range(NX):
             CC[t] = dot(G[t], pick)
-        local_wait(W.at[0, 1 - c], rP.at[0])
-        for k in range(NX):
-            W1[:, :, 128 * k : 128 * k + 128, :] = W[0, :, :, BLK * k : BLK * k + 128, :]
-            W1[:, :, 512 + 32 * k : 544 + 32 * k, :] = W[0, :, :, BLK * k + 128 : BLK * k + BLK, :]
 
     local_wait(G.at[0:3], rG)
     local_wait(W.at[1, 1 - c], rP.at[1])
     conv(0, 1, mul_cot)
+    ring_step(0, 0)
     mean = take_sums(0)
     stats = []
     for a in range(2):
@@ -378,6 +399,11 @@
         Gh[x, 512 + 64 * img : 576 + 64 * img, :] = rest.astype(BF16)
     for k in range(1, NX):
         remote(Gh.at[x], Gh.at[x], sGh, rGh, dev(lax.rem(x + k, NX), y, z, c)).start()
+    ring_step(0, 3)
+    local_wait(W.at[0, 1 - c], rP.at[0])
+    for k in range(NX):
+        W1[:, :, 128 * k : 128 * k + 128, :] = W[0, :, :, BLK * k : BLK * k + 128, :]
+        W1[:, :, 512 + 32 * k : 544 + 32 * k, :] = W[0, :, :, BLK * k + 128 : BLK * k + BLK, :]
     local_wait(Gh.at[0:3], rGh)
     lane = iota((PX, 128), 1)
     rests = [Gh[k, 512:640, :].astype(F32) for k in range(NX)]
@@ -393,20 +419,17 @@
     conv(1, 0, mul_grad)
     first, second = norm_sums(2, 1, params[2], params[3])
     for t in range(NX):
-        for img in range(2):
-            q = slice(64 * img, 64 * img + 64)
-            v = CC[t, q, :] + norm_apply(1, t, img, first, second)
-            Os[t, q, :] = v.astype(BF16)
+        v = jnp.concatenate([norm_apply(1, t, img, first, second) for img in range(2)], axis=0)
+        Os[t] = pack(CC[t] + v).astype(BF16)
     for k in range(1, NX):
         t = lax.rem(x + k, NX)
         remote(Os.at[t], Oc.at[x], sO, rO, dev(t, y, z, c)).start()
     Oc[x] = Os[x]
 
     for f in (1, 0):
-        mine = mine_y if f == 1 else mine_z
         local_wait(RA.at[f, 0:7], sA.at[f])
 
-        @pl.when(jnp.logical_not(mine))
+        @pl.when(jnp.logical_not(mine[f]))
         def _():
             local_wait(RA.at[f, 0], sA0.at[f])
 
@@ -428,9 +451,9 @@
 
     local_wait(Oc.at[0:3], rO)
     local_wait(Oc.at[0:3], sO)
-    out[...] = jnp.concatenate([Oc[k, :, 0:BLK].astype(F32) for k in range(NX)], axis=1).astype(
-        BF16
-    )
+    out[...] = jnp.concatenate(
+        [unpack(Oc[k].astype(F32))[:, 0:BLK] for k in range(NX)], axis=1
+    ).astype(BF16)
 
 
 def body(latent, hidden, cotangent, filter_one, filter_two, gain_one, shift_one, gain_two, shift_two):
@@ -449,10 +472,10 @@
             pltpu.VMEM((2, 9, 20, 40), BF16),
             [pltpu.VMEM((CH,), F32)] * 4,
             pltpu.VMEM((2, PX, CH), BF16),
-            pltpu.VMEM((2, 32, 384), BF16),
+            pltpu.VMEM((2, 24, 384), BF16),
             pltpu.VMEM((2, 2, 3, CH, 256), BF16),
             pltpu.VMEM((2, 3, CH, 256), BF16),
-            pltpu.VMEM((2, 8, 32, 384), BF16),
+            pltpu.VMEM((2, 8, 24, 384), BF16),
             pltpu.VMEM((NX, PX, CH), BF16),
             pltpu.VMEM((NX, 640, 128), BF16),
             pltpu.VMEM((NX * PX, CH), BF16),
@@ -461,12 +484,12 @@
             pltpu.VMEM((2, NX, PX, 256), F32),
             pltpu.VMEM((3, 8, 256), F32),
             pltpu.VMEM((3, NY, 8, 256), F32),
-            pltpu.VMEM((2, 2, PX, 256), F32),
-            pltpu.VMEM((2, 2, PX, 256), F32),
+            pltpu.VMEM((2, 2, BLK, 128), F32),
+            pltpu.VMEM((2, 2, BLK, 128), F32),
             pltpu.VMEM((2, NX * PX, 256), F32),
             pltpu.VMEM((NX * PX, 256), F32),
-            pltpu.VMEM((NX, PX, 256), BF16),
-            pltpu.VMEM((NX, PX, 256), BF16),
+            pltpu.VMEM((NX, BLK, 128), BF16),
+            pltpu.VMEM((NX, BLK, 128), BF16),
             pltpu.VMEM((NX, PX, 256), F32),
             dma((2,)), dma((4,)), dma((2,)), dma,
             dma((2,)), dma((2,)), dma((2,)),

time: 82.7 us -> 77.5 us (0.937)
  the two profiles are of different devices: /device:TPU:8 before, /device:TPU:4 now
where the time goes in v3:
time: 77.5 us; the launch traced here: 77.3 us
  Pallas kernels  75.7 us (98%)
  local copies, waits for them, and re-layouts  1.6 us (2%)
    pallas_call x1, Pallas kernels, body(): pl.pallas_call(kernel, out_shape=jax.ShapeDtypeStruct((PX, CH), BF16), in...  75.7 us
    unnamed x1, local copies, waits for them, and re-layouts  1.6 us

profile of v3, /device:TPU:4, one launch (start us, length us, event | category | flops | bytes accessed | tf_op | source)
XLA Modules:
  0.0 77.3 jit_solution(2694449736035653428)
XLA Ops:
  0.0 75.7 %block_backward.1 = bf16[128,640]{1,0:T(8,128)(2,1)} custom-call(bf16[9,20,40]{2,1,0:T(8,128)(2,1)} %bitcast.12, bf16[9,20,40]{2,1,0:T(8,128)(2,1)} %bitcast.13, bf16[128,640]{1,0:T(8,128)(2,1)} %bitcast.9, bf16[128,640]{1,0:T(8,128)(2,1)} %bitcast.10, bf16[128,640]{1,0:T(8,128)(2,1)} %bitcast.11, f32[640]{0:T(1024)} %g2.1, f32[640]{0:T(1024)} %s2_.1, ...), custom_call_target="tpu_custom_call" | custom-call | tf_op jit(solution)/shard_map/block_backward/pallas_call | solution.py:466
  75.7 1.6 %copy.12 = bf16[2,1,64,640]{3,2,1,0:T(8,128)(2,1)} copy(bf16[2,1,64,640]{3,2,1,0:T(8,128)(2,1)} %bitcast.8) | data formatting | bytes 327680

commit v4 on v3

--- a/solution.py
+++ b/solution.py
@@ -36,8 +36,8 @@
 
 def kernel(
     f1, f2, cot, hid, lat, g2, s2, g1, s1, out,
-    FV, PV, HV, WB, W, W1, RA, G, Gh, L, Hs, Hc, Hx, SS, ST, HBs, HBr, AC, BK, Os, Oc, CC,
-    lF, lP, lH, lC, sA, sA0, rA, sR, rR, sP, rP, sG, rG, sGh, rGh, sH, rH, sS, rS, sB, rB, sO, rO,
+    FV, PV, HV, WB, W, W1, RA, G, Gh, L, Hs, Hc, Hx, SS, ST, Hb, HxB, PB, KB, HBs, HBr, AC, BK, Os, Oc, CC,
+    lF, lP, lH, lC, sA, sA0, rA, sR, rR, sP, rP, sG, rG, sGh, rGh, sH, rH, sS, rS, sB, rB, sO, rO, sN, rN,
 ):
     dp = lax.axis_index("dp")
     rr = lax.axis_index("rows")
@@ -58,6 +58,7 @@
     def local_wait(ref, sem):
         pltpu.make_async_copy(ref, ref, sem).wait()
 
+    Hb[...] = jnp.zeros_like(Hb)
     bar = pltpu.get_barrier_semaphore()
 
     def here(target):
@@ -82,7 +83,7 @@
         here(dev(lax.rem(x + k, NX), y, z, c))
     for k in range(1, NY):
         here(dev(x, lax.rem(y + k, NY), z, c))
-    for k in (1, NZ - 1):
+    for k in (1, 2, NZ - 2, NZ - 1):
         here(dev(x, y, lax.rem(z + k, NZ), c))
     here(dev(x, y, z, 1 - c))
 
@@ -122,7 +123,7 @@
     own_cot.wait()
 
     pl.semaphore_wait(
-        bar, 29 - mine_y.astype(jnp.int32) - mine_z.astype(jnp.int32)
+        bar, 31 - mine_y.astype(jnp.int32) - mine_z.astype(jnp.int32)
     )
 
     slot = lax.rem(z, 2) * 4 + x
@@ -149,10 +150,10 @@
     first_stage(1)
     for k in range(1, NX):
         t = lax.rem(x + k, NX)
-        remote(G.at[x], G.at[x], sG, rG, dev(t, y, z, c)).start()
+        remote(Hs.at[t], Hc.at[x], sH, rH, dev(t, y, z, c)).start()
     for k in range(1, NX):
         t = lax.rem(x + k, NX)
-        remote(Hs.at[t], Hc.at[x], sH, rH, dev(t, y, z, c)).start()
+        remote(G.at[x], G.at[x], sG, rG, dev(t, y, z, c)).start()
     Hc[x] = Hs[x]
 
     def region(f, cc, a, o):
@@ -173,20 +174,13 @@
     def at(f, p):
         return dev(x, jnp.where(along_y[f], p, y), jnp.where(along_y[f], z, p), c)
 
-    def up(f, s, a):
+    def ring(f, way, step, a, hops):
         p = place[f]
-        o = lax.rem(p - s + 8, 8)
+        sign = 1 if way == 0 else -1
+        o = lax.rem(p - sign * (step + 1 - hops) + 8, 8)
         return remote(
-            region(f, c, a, o), region(f, c, a, o), sR.at[f], rR.at[f, 0, s, a],
-            at(f, lax.rem(p + 1, 8)),
-        )
-
-    def down(f, s, a):
-        p = place[f]
-        o = lax.rem(p + s, 8)
-        return remote(
-            region(f, c, a, o), region(f, c, a, o), sR.at[f], rR.at[f, 1, s, a],
-            at(f, lax.rem(p + 7, 8)),
+            region(f, c, a, o), region(f, c, a, o), sR.at[f], rR.at[f, way, step, a],
+            at(f, lax.rem(p + sign * hops + 8, 8)),
         )
 
     def share(f, a, o):
@@ -204,30 +198,41 @@
                     f, c, a, pl.ds(pl.multiple_of(80 * place[f], 16), 80),
                     128 * b : 128 * b + 128,
                 ] = piece[:, 128 * a : 128 * a + 128]
+        for hops in (2, 1):
+            for a in range(3):
+                for way in range(2):
+                    ring(f, way, hops - 1, a, hops).start()
         for a in range(3):
-            up(f, 0, a).start()
-            down(f, 0, a).start()
             share(f, a, place[f])
 
     def ring_step(f, s):
+        step = (1, 0, 2, 3)[s]
         for a in range(3):
-            up(f, s, a).wait_recv()
-            if s < 3:
-                up(f, s + 1, a).start()
-            share(f, a, place[f] - 1 - s)
-            if s < 3:
-                down(f, s, a).wait_recv()
-                if s < 2:
-                    down(f, s + 1, a).start()
-                share(f, a, place[f] + 1 + s)
+            for way in range(2):
+                if step == 3 and way != a % 2:
+                    continue
+                ring(f, way, step, a, 0).wait_recv()
+                if step == 1:
+                    ring(f, way, 2, a, 1).start()
+                    if way == a % 2:
+                        ring(f, way, 3, a, 2).start()
+                share(f, a, place[f] - (step + 1) * (1 if way == 0 else -1))
 
     start_ring(1)
     first_stage(0)
-    for s in range(4):
+    for s in range(2):
         ring_step(1, s)
 
     row8 = iota((8, 256), 0)
     local_wait(Hc.at[0:3], rH)
+    @pl.when(y < NY - 1)
+    def _():
+        remote(Hc.at[3], Hb.at[0], sN.at[0], rN.at[0], dev(x, lax.rem(y + 1, 8), z, c)).start()
+
+    @pl.when(y > 0)
+    def _():
+        remote(Hc.at[0], Hb.at[1], sN.at[1], rN.at[1], dev(x, lax.rem(y + 7, 8), z, c)).start()
+
     zero = jnp.zeros((64, 256 - BLK), F32)
     sums = jnp.zeros((8, 256), F32)
     for img in range(2):
@@ -264,6 +269,8 @@
         return dot(tot, same, precision=lax.Precision.HIGHEST) / NUMBER
 
     send_sums(0, sums)
+    for s in range(2, 4):
+        ring_step(1, s)
     start_ring(0)
 
     ln128 = iota((32, 128), 1)
@@ -305,7 +312,8 @@
 
     def conv(n, f, mul):
         for e, (ai, t) in enumerate(((0, 0), (2, 3))):
-            HBs[n, e] = pack(combine([mul(f, cc, ai, t, t + 1) for cc in range(2)]))
+            PB[e] = combine([mul(f, cc, ai, t, t + 1) for cc in range(2)])
+            HBs[n, e] = pack(PB[e])
 
         @pl.when(y > 0)
         def _():
@@ -326,7 +334,7 @@
         def _():
             local_wait(HBr.at[n, e], rB.at[n, e])
             px = slice(384, 512) if e == 0 else slice(0, 128)
-            BK[px] += unpack(HBr[n, e])
+            BK[px] += unpack(HBr[n, e]) * KB[1 - e]
 
     def mul_cot(f, cc, ai, t0, t1):
         return dot(G[t0:t1].reshape((t1 - t0) * PX, CH), W[f, cc, ai])
@@ -338,19 +346,22 @@
         avg, inv = stats[a]
         first = [jnp.zeros((1, 256), F32)] * 2
         second = [jnp.zeros((1, 256), F32)] * 2
-        for t in (1, 2, 0, 3):
-            if t == 0:
-                take_halo(n - 1, 1)
-            if t == 3:
-                take_halo(n - 1, 0)
+        for t in (0, 1, 2, 3, 4, 5):
             for img in range(2):
+                q = slice(64 * img, 64 * img + 64)
                 px = slice(t * PX + 64 * img, t * PX + 64 * img + 64)
-                v = Hx[a, t, 64 * img : 64 * img + 64, :]
+                v = Hx[a, t, q, :] if t < 4 else HxB[a, t - 4, q, :]
                 normed = (v - avg[img : img + 1]) * inv[img : img + 1]
                 linear = normed * gain + shift
                 s = jax.nn.sigmoid(linear)
-                scaled = BK[px, :] * s * (1.0 + linear * (1.0 - s)) * gain
-                BK[px, :] = scaled
+                slope = s * (1.0 + linear * (1.0 - s)) * gain
+                if t < 4:
+                    scaled = BK[px, :] * slope
+                    BK[px, :] = scaled
+                    if t in (0, 3):
+                        KB[t // 3, q, :] = slope
+                else:
+                    scaled = jnp.where(y > 0 if t == 4 else y < NY - 1, PB[t - 4, q, :] * slope, 0.0)
                 first[img] = first[img] + jnp.sum(scaled, axis=0, keepdims=True)
                 second[img] = second[img] + jnp.sum(scaled * normed, axis=0, keepdims=True)
         value = jnp.zeros((8, 256), F32)
@@ -359,9 +370,10 @@
             value = jnp.where(row8 == 2 + img, second[img], value)
         send_sums(n, value)
         if n == 1:
-            ring_step(0, 1)
             spare_time()
-            ring_step(0, 2)
+            ring_step(0, 0)
+        take_halo(n - 1, 1)
+        take_halo(n - 1, 0)
         got = take_sums(n)
         return got[0:2], got[2:4]
 
@@ -382,13 +394,26 @@
     local_wait(G.at[0:3], rG)
     local_wait(W.at[1, 1 - c], rP.at[1])
     conv(0, 1, mul_cot)
-    ring_step(0, 0)
     mean = take_sums(0)
     stats = []
     for a in range(2):
         avg = mean[4 * a : 4 * a + 2]
         inv = lax.rsqrt(mean[4 * a + 2 : 4 * a + 4] - avg * avg + 1e-05)
         stats.append((avg, inv))
+    @pl.when(y > 0)
+    def _():
+        local_wait(Hb.at[0], rN.at[0])
+
+    @pl.when(y < NY - 1)
+    def _():
+        local_wait(Hb.at[1], rN.at[1])
+
+    for e in range(2):
+        both = Hb[e].astype(F32)
+        for a in range(2):
+            HxB[a, e] = jnp.concatenate(
+                [both[:, BLK * a : BLK * a + BLK], jnp.zeros((PX, 256 - BLK), F32)], axis=1
+            )
     first, second = norm_sums(1, 0, params[0], params[1])
     for img in range(2):
         rest = jnp.zeros((64, 128), F32)
@@ -399,7 +424,8 @@
         Gh[x, 512 + 64 * img : 576 + 64 * img, :] = rest.astype(BF16)
     for k in range(1, NX):
         remote(Gh.at[x], Gh.at[x], sGh, rGh, dev(lax.rem(x + k, NX), y, z, c)).start()
-    ring_step(0, 3)
+    for s in range(1, 4):
+        ring_step(0, s)
     local_wait(W.at[0, 1 - c], rP.at[0])
     for k in range(NX):
         W1[:, :, 128 * k : 128 * k + 128, :] = W[0, :, :, BLK * k : BLK * k + 128, :]
@@ -438,6 +464,15 @@
     local_wait(G.at[0:3], sG)
     local_wait(Gh.at[0:3], sGh)
     local_wait(Hc.at[0:3], sH)
+
+    @pl.when(y < NY - 1)
+    def _():
+        local_wait(Hc.at[3], sN.at[0])
+
+    @pl.when(y > 0)
+    def _():
+        local_wait(Hc.at[0], sN.at[1])
+
     for p in range(3):
         local_wait(ST.at[p, 0:7], sS.at[p])
     for n in range(2):
@@ -484,6 +519,10 @@
             pltpu.VMEM((2, NX, PX, 256), F32),
             pltpu.VMEM((3, 8, 256), F32),
             pltpu.VMEM((3, NY, 8, 256), F32),
+            pltpu.VMEM((2, PX, 384), BF16),
+            pltpu.VMEM((2, 2, PX, 256), F32),
+            pltpu.VMEM((2, PX, 256), F32),
+            pltpu.VMEM((2, PX, 256), F32),
             pltpu.VMEM((2, 2, BLK, 128), F32),
             pltpu.VMEM((2, 2, BLK, 128), F32),
             pltpu.VMEM((2, NX * PX, 256), F32),
@@ -499,6 +538,7 @@
             dma((3,)), dma((3,)),
             dma((2, 2)), dma((2, 2)),
             dma, dma,
+            dma((2,)), dma((2,)),
         ],
         compiler_params=pltpu.CompilerParams(
             collective_id=0, has_side_effects=True, vmem_limit_bytes=62 * 1024 * 1024

time: 77.5 us -> 71 us (0.916)
  the two profiles are of different devices: /device:TPU:4 before, /device:TPU:1 now
where the time goes in v4:
time: 71 us; the launch traced here: 70.8 us
  Pallas kernels  69.2 us (97%)
  local copies, waits for them, and re-layouts  1.6 us (2%)
    pallas_call x1, Pallas kernels, body(): pl.pallas_call(kernel, out_shape=jax.ShapeDtypeStruct((PX, CH), BF16), in...  69.2 us
    unnamed x1, local copies, waits for them, and re-layouts  1.6 us

profile of v4, /device:TPU:1, one launch (start us, length us, event | category | flops | bytes accessed | tf_op | source)
XLA Modules:
  0.0 70.8 jit_solution(8632076149456304483)
XLA Ops:
  0.0 69.2 %block_backward.1 = bf16[128,640]{1,0:T(8,128)(2,1)} custom-call(bf16[9,20,40]{2,1,0:T(8,128)(2,1)} %bitcast.12, bf16[9,20,40]{2,1,0:T(8,128)(2,1)} %bitcast.13, bf16[128,640]{1,0:T(8,128)(2,1)} %bitcast.9, bf16[128,640]{1,0:T(8,128)(2,1)} %bitcast.10, bf16[128,640]{1,0:T(8,128)(2,1)} %bitcast.11, f32[640]{0:T(1024)} %g2.1, f32[640]{0:T(1024)} %s2_.1, ...), custom_call_target="tpu_custom_call" | custom-call | tf_op jit(solution)/shard_map/block_backward/pallas_call | solution.py:501
  69.2 1.6 %copy.12 = bf16[2,1,64,640]{3,2,1,0:T(8,128)(2,1)} copy(bf16[2,1,64,640]{3,2,1,0:T(8,128)(2,1)} %bitcast.8) | data formatting | bytes 327680

commit v5 on v4

--- a/solution.py
+++ b/solution.py
@@ -36,7 +36,7 @@
 
 def kernel(
     f1, f2, cot, hid, lat, g2, s2, g1, s1, out,
-    FV, PV, HV, WB, W, W1, RA, G, Gh, L, Hs, Hc, Hx, SS, ST, Hb, HxB, PB, KB, HBs, HBr, AC, BK, Os, Oc, CC,
+    FV, PV, HV, WB, W, W1, RA, G, Gh, L, Hs, Hc, Hx, SS, ST, Hb, HxB, NB, SB, PB, KB, HBs, HBr, AC, BK, Os, Oc, CC,
     lF, lP, lH, lC, sA, sA0, rA, sR, rR, sP, rP, sG, rG, sGh, rGh, sH, rH, sS, rS, sB, rB, sO, rO, sN, rN,
 ):
     dp = lax.axis_index("dp")
@@ -97,30 +97,16 @@
         load.start()
     own_cot.start()
     WB[...] = jnp.zeros_like(WB)
-    for f in (1, 0):
+
+    def own_block(f):
         loads[f].wait()
         for a in range(3):
             taps = [FV[f, 3 * a + b].astype(F32) for b in range(3)]
             WB[f, 0:20, 128 * a : 128 * a + 128] = jnp.concatenate(
                 taps + [jnp.zeros((20, 8), F32)], axis=1
             ).astype(BF16)
-    for a in range(2):
-        loads[2 + a].wait()
-    v = [HV[a].astype(F32) for a in range(2)]
-    for k in range(NX):
-        Hs[k] = jnp.concatenate(
-            [v[a][:, BLK * k : BLK * k + BLK] for a in range(2)] + [jnp.zeros((PX, 64), F32)],
-            axis=1,
-        ).astype(BF16)
-    params = []
-    for a in range(4):
-        loads[4 + a].wait()
-        whole = PV[a][...].reshape(1, CH)
-        p = jnp.zeros((1, BLK), F32)
-        for k in range(NX):
-            p = jnp.where(x == k, whole[:, BLK * k : BLK * k + BLK], p)
-        params.append(jnp.concatenate([p, jnp.zeros((1, 256 - BLK), F32)], axis=1))
-    own_cot.wait()
+
+    own_block(1)
 
     pl.semaphore_wait(
         bar, 31 - mine_y.astype(jnp.int32) - mine_z.astype(jnp.int32)
@@ -148,6 +134,15 @@
                 remote(WB.at[f], RA.at[f, slot], sA.at[f], rA.at[f], target).start()
 
     first_stage(1)
+    for a in range(2):
+        loads[2 + a].wait()
+    v = [HV[a].astype(F32) for a in range(2)]
+    for k in range(NX):
+        Hs[k] = jnp.concatenate(
+            [v[a][:, BLK * k : BLK * k + BLK] for a in range(2)] + [jnp.zeros((PX, 64), F32)],
+            axis=1,
+        ).astype(BF16)
+    own_cot.wait()
     for k in range(1, NX):
         t = lax.rem(x + k, NX)
         remote(Hs.at[t], Hc.at[x], sH, rH, dev(t, y, z, c)).start()
@@ -155,6 +150,15 @@
         t = lax.rem(x + k, NX)
         remote(G.at[x], G.at[x], sG, rG, dev(t, y, z, c)).start()
     Hc[x] = Hs[x]
+    own_block(0)
+    params = []
+    for a in range(4):
+        loads[4 + a].wait()
+        whole = PV[a][...].reshape(1, CH)
+        p = jnp.zeros((1, BLK), F32)
+        for k in range(NX):
+            p = jnp.where(x == k, whole[:, BLK * k : BLK * k + BLK], p)
+        params.append(jnp.concatenate([p, jnp.zeros((1, 256 - BLK), F32)], axis=1))
 
     def region(f, cc, a, o):
         return W.at[f, cc, a, pl.ds(pl.multiple_of(80 * o, 16), 80), :]
@@ -249,7 +253,21 @@
             sums = jnp.where(row8 == 4 * a + img, tot[a], sums)
             sums = jnp.where(row8 == 4 * a + 2 + img, sq[a], sums)
 
+    gi = group_of(iota((256, 256), 0))
+    gj = group_of(iota((256, 256), 1))
+    same = jnp.logical_and(gi == gj, gi < 4).astype(F32).astype(BF16)
+
+    def group_totals(v):
+        high = v.astype(BF16)
+        left = v - high.astype(F32)
+        mid = left.astype(BF16)
+        low = (left - mid.astype(F32)).astype(BF16)
+        terms = jnp.concatenate([high.astype(F32), mid.astype(F32), low.astype(F32)], axis=0).astype(BF16)
+        got = dot(terms, same[:, 0:128])
+        return got[0:8] + got[8:16] + got[16:24]
+
     def send_sums(p, value):
+        value = group_totals(value)
         SS[p] = value
         ST[p, y] = value
         for k in range(1, NY):
@@ -257,16 +275,14 @@
                 SS.at[p], ST.at[p, y], sS.at[p], rS.at[p], dev(x, lax.rem(y + k, NY), z, c)
             ).start()
 
-    gi = group_of(iota((256, 256), 0))
-    gj = group_of(iota((256, 256), 1))
-    same = jnp.logical_and(gi == gj, gi < 4).astype(F32)
-
     def take_sums(p):
         local_wait(ST.at[p, 0:7], rS.at[p])
         tot = ST[p, 0]
         for k in range(1, NY):
             tot = tot + ST[p, k]
-        return dot(tot, same, precision=lax.Precision.HIGHEST) / NUMBER
+        tot = tot * (1.0 / NUMBER)
+        last = jnp.where(iota((8, 128), 1) < 32, tot[:, 127:128], 0.0)
+        return jnp.concatenate([tot, last], axis=1)
 
     send_sums(0, sums)
     for s in range(2, 4):
@@ -294,20 +310,21 @@
         ln = iota((rows, 128), 1)
         t0 = jnp.zeros((rows, 128), F32)
         t1 = jnp.zeros((rows, 128), F32)
-        for j in range(4):
-            b = j // 2
-            blk = accs[j % 2][:, 128 * b : 128 * b + 128]
-            low = jnp.where(q == 63, 0.0, pltpu.roll(blk, rows - 1, 0))
-            mid = pltpu.roll(blk, 128 - 40, 1)
-            high = jnp.where(q == 0, 0.0, pltpu.roll(pltpu.roll(blk, 128 - 80, 1), 1, 0))
-            v = jnp.where(ln < 40, low + mid + high, 0.0)
-            if j:
-                v = pltpu.roll(v, 40 * j, 1)
-            if j < 3:
-                t0 = t0 + v
-            else:
-                t0 = t0 + jnp.where(ln >= 120, v, 0.0)
-                t1 = jnp.where(ln < 32, v, 0.0)
+        for p in range(3):
+            r = []
+            for j in range(4):
+                b = j // 2
+                blk = accs[j % 2][:, 128 * b : 128 * b + 128]
+                shift = (40 * j - 40 * p) % 128
+                r.append(pltpu.roll(blk, shift, 1) if shift else blk)
+            u0 = jnp.where(ln < 40, r[0], jnp.where(ln < 80, r[1], jnp.where(ln < 120, r[2], r[3])))
+            u1 = jnp.where(ln < 32, r[3], 0.0)
+            if p == 0:
+                u0, u1 = (jnp.where(q == 63, 0.0, pltpu.roll(u, rows - 1, 0)) for u in (u0, u1))
+            if p == 2:
+                u0, u1 = (jnp.where(q == 0, 0.0, pltpu.roll(u, 1, 0)) for u in (u0, u1))
+            t0 = t0 + u0
+            t1 = t1 + u1
         return jnp.concatenate([t0, t1], axis=1)
 
     def conv(n, f, mul):
@@ -342,19 +359,26 @@
     def mul_grad(f, cc, ai, t0, t1):
         return dot(L[t0 * PX : t1 * PX, :], W1[cc, ai])
 
+    def slopes(a, t, img, gain, shift):
+        avg, inv = stats[a]
+        q = slice(64 * img, 64 * img + 64)
+        v = Hx[a, t, q, :] if t < 4 else HxB[a, t - 4, q, :]
+        normed = (v - avg[img : img + 1]) * inv[img : img + 1]
+        linear = normed * gain + shift
+        s = jax.nn.sigmoid(linear)
+        return normed, s * (1.0 + linear * (1.0 - s)) * gain
+
     def norm_sums(n, a, gain, shift):
-        avg, inv = stats[a]
         first = [jnp.zeros((1, 256), F32)] * 2
         second = [jnp.zeros((1, 256), F32)] * 2
-        for t in (0, 1, 2, 3, 4, 5):
+        for t in range(6):
             for img in range(2):
                 q = slice(64 * img, 64 * img + 64)
                 px = slice(t * PX + 64 * img, t * PX + 64 * img + 64)
-                v = Hx[a, t, q, :] if t < 4 else HxB[a, t - 4, q, :]
-                normed = (v - avg[img : img + 1]) * inv[img : img + 1]
-                linear = normed * gain + shift
-                s = jax.nn.sigmoid(linear)
-                slope = s * (1.0 + linear * (1.0 - s)) * gain
+                if n == 1:
+                    normed, slope = slopes(a, t, img, gain, shift)
+                else:
+                    normed, slope = NB[t, q, :], SB[t, q, :]
                 if t < 4:
                     scaled = BK[px, :] * slope
                     BK[px, :] = scaled
@@ -430,6 +454,10 @@
     for k in range(NX):
         W1[:, :, 128 * k : 128 * k + 128, :] = W[0, :, :, BLK * k : BLK * k + 128, :]
         W1[:, :, 512 + 32 * k : 544 + 32 * k, :] = W[0, :, :, BLK * k + 128 : BLK * k + BLK, :]
+    for t in range(6):
+        for img in range(2):
+            q = slice(64 * img, 64 * img + 64)
+            NB[t, q, :], SB[t, q, :] = slopes(1, t, img, params[2], params[3])
     local_wait(Gh.at[0:3], rGh)
     lane = iota((PX, 128), 1)
     rests = [Gh[k, 512:640, :].astype(F32) for k in range(NX)]
@@ -517,10 +545,12 @@
             pltpu.VMEM((NX, PX, 384), BF16),
             pltpu.VMEM((NX, PX, 384), BF16),
             pltpu.VMEM((2, NX, PX, 256), F32),
-            pltpu.VMEM((3, 8, 256), F32),
-            pltpu.VMEM((3, NY, 8, 256), F32),
+            pltpu.VMEM((3, 8, 128), F32),
+            pltpu.VMEM((3, NY, 8, 128), F32),
             pltpu.VMEM((2, PX, 384), BF16),
             pltpu.VMEM((2, 2, PX, 256), F32),
+            pltpu.VMEM((6, PX, 256), F32),
+            pltpu.VMEM((6, PX, 256), F32),
             pltpu.VMEM((2, PX, 256), F32),
             pltpu.VMEM((2, PX, 256), F32),
             pltpu.VMEM((2, 2, BLK, 128), F32),

time: 71 us -> 68.8 us (0.969)
  Pallas kernels: 69.2 us -> 67 us
    pallas_call x1, Pallas kernels: 69.2 us -> 67 us  [body(): pl.pallas_call(kernel, out_shape=jax.ShapeDtypeStruct((PX, CH), BF16), in...]
where the time goes in v5:
time: 68.8 us; the launch traced here: 68.6 us
  Pallas kernels  67 us (97%)
  local copies, waits for them, and re-layouts  1.6 us (2%)
    pallas_call x1, Pallas kernels, body(): pl.pallas_call(kernel, out_shape=jax.ShapeDtypeStruct((PX, CH), BF16), in...  67 us
    unnamed x1, local copies, waits for them, and re-layouts  1.6 us

profile of v5, /device:TPU:1, one launch (start us, length us, event | category | flops | bytes accessed | tf_op | source)
XLA Modules:
  0.0 68.6 jit_solution(15551509702605370636)
XLA Ops:
  0.0 67.0 %block_backward.1 = bf16[128,640]{1,0:T(8,128)(2,1)} custom-call(bf16[9,20,40]{2,1,0:T(8,128)(2,1)} %bitcast.12, bf16[9,20,40]{2,1,0:T(8,128)(2,1)} %bitcast.13, bf16[128,640]{1,0:T(8,128)(2,1)} %bitcast.9, bf16[128,640]{1,0:T(8,128)(2,1)} %bitcast.10, bf16[128,640]{1,0:T(8,128)(2,1)} %bitcast.11, f32[640]{0:T(1024)} %g2.1, f32[640]{0:T(1024)} %s2_.1, ...), custom_call_target="tpu_custom_call" | custom-call | tf_op jit(solution)/shard_map/block_backward/pallas_call | solution.py:529
  67.0 1.6 %copy.12 = bf16[2,1,64,640]{3,2,1,0:T(8,128)(2,1)} copy(bf16[2,1,64,640]{3,2,1,0:T(8,128)(2,1)} %bitcast.8) | data formatting | bytes 327680

commit v6 on v5

--- a/solution.py
+++ b/solution.py
@@ -289,20 +289,20 @@
         ring_step(1, s)
     start_ring(0)
 
-    ln128 = iota((32, 128), 1)
+    ln128 = iota((16, 128), 1)
 
     def pack(v):
-        fold = v[0:32, 128:256]
+        fold = v[0:16, 128:256]
         for g in range(1, 4):
-            fold = fold + pltpu.roll(v[32 * g : 32 * g + 32, 128:256], 32 * g, 1)
+            fold = fold + pltpu.roll(v[16 * g : 16 * g + 16, 128:256], 32 * g, 1)
         return jnp.concatenate([v[:, 0:128], fold], axis=0)
 
     def unpack(m):
-        fold = m[128:160]
+        fold = m[64:80]
         rest = [jnp.where(ln128 < 32, fold, 0.0)]
         for g in range(1, 4):
             rest.append(jnp.where(ln128 < 32, pltpu.roll(fold, 128 - 32 * g, 1), 0.0))
-        return jnp.concatenate([m[0:128], jnp.concatenate(rest, axis=0)], axis=1)
+        return jnp.concatenate([m[0:64], jnp.concatenate(rest, axis=0)], axis=1)
 
     def combine(accs):
         rows = accs[0].shape[0]
@@ -327,97 +327,88 @@
             t1 = t1 + u1
         return jnp.concatenate([t0, t1], axis=1)
 
-    def conv(n, f, mul):
+    def conv(n, img, mul):
+        for cc in range(2):
+            AC[cc] = mul(img, cc, 1, 0, 4)
+            AC[cc, 0:192] += mul(img, cc, 0, 1, 4)
+            AC[cc, 64:256] += mul(img, cc, 2, 0, 3)
+        BK[img] = combine([AC[0], AC[1]])
         for e, (ai, t) in enumerate(((0, 0), (2, 3))):
-            PB[e] = combine([mul(f, cc, ai, t, t + 1) for cc in range(2)])
-            HBs[n, e] = pack(PB[e])
+            PB[img, e] = combine([mul(img, cc, ai, t, t + 1) for cc in range(2)])
+            HBs[n, img, e] = pack(PB[img, e])
 
         @pl.when(y > 0)
         def _():
-            remote(HBs.at[n, 0], HBr.at[n, 0], sB.at[n, 0], rB.at[n, 0], dev(x, lax.rem(y + 7, 8), z, c)).start()
+            remote(
+                HBs.at[n, img, 0], HBr.at[n, img, 0], sB.at[n, img, 0], rB.at[n, img, 0],
+                dev(x, lax.rem(y + 7, 8), z, c),
+            ).start()
 
         @pl.when(y < NY - 1)
         def _():
-            remote(HBs.at[n, 1], HBr.at[n, 1], sB.at[n, 1], rB.at[n, 1], dev(x, lax.rem(y + 1, 8), z, c)).start()
-
-        for cc in range(2):
-            AC[cc] = mul(f, cc, 1, 0, 4)
-            AC[cc, 0:384] += mul(f, cc, 0, 1, 4)
-            AC[cc, 128:512] += mul(f, cc, 2, 0, 3)
-        BK[...] = combine([AC[0], AC[1]])
-
-    def take_halo(n, e):
+            remote(
+                HBs.at[n, img, 1], HBr.at[n, img, 1], sB.at[n, img, 1], rB.at[n, img, 1],
+                dev(x, lax.rem(y + 1, 8), z, c),
+            ).start()
+
+    def take_halo(n, img, e):
         @pl.when(y < NY - 1 if e == 0 else y > 0)
         def _():
-            local_wait(HBr.at[n, e], rB.at[n, e])
-            px = slice(384, 512) if e == 0 else slice(0, 128)
-            BK[px] += unpack(HBr[n, e]) * KB[1 - e]
-
-    def mul_cot(f, cc, ai, t0, t1):
-        return dot(G[t0:t1].reshape((t1 - t0) * PX, CH), W[f, cc, ai])
-
-    def mul_grad(f, cc, ai, t0, t1):
-        return dot(L[t0 * PX : t1 * PX, :], W1[cc, ai])
-
-    def slopes(a, t, img, gain, shift):
-        avg, inv = stats[a]
+            local_wait(HBr.at[n, img, e], rB.at[n, img, e])
+            px = slice(192, 256) if e == 0 else slice(0, 64)
+            BK[img, px] += unpack(HBr[n, img, e]) * KB[img, 1 - e]
+
+    def mul_cot(img, cc, ai, t0, t1):
+        rows = G[t0:t1, 64 * img : 64 * img + 64, :].reshape((t1 - t0) * 64, CH)
+        return dot(rows, W[1, cc, ai])
+
+    def mul_grad(img, cc, ai, t0, t1):
+        return dot(L[img, 64 * t0 : 64 * t1, :], W1[cc, ai])
+
+    def slopes(a, img):
+        avg, inv = (v[img : img + 1] for v in stats[a])
+        gain, shift = params[2 * a], params[2 * a + 1]
         q = slice(64 * img, 64 * img + 64)
-        v = Hx[a, t, q, :] if t < 4 else HxB[a, t - 4, q, :]
-        normed = (v - avg[img : img + 1]) * inv[img : img + 1]
-        linear = normed * gain + shift
-        s = jax.nn.sigmoid(linear)
-        return normed, s * (1.0 + linear * (1.0 - s)) * gain
-
-    def norm_sums(n, a, gain, shift):
-        first = [jnp.zeros((1, 256), F32)] * 2
-        second = [jnp.zeros((1, 256), F32)] * 2
         for t in range(6):
-            for img in range(2):
-                q = slice(64 * img, 64 * img + 64)
-                px = slice(t * PX + 64 * img, t * PX + 64 * img + 64)
-                if n == 1:
-                    normed, slope = slopes(a, t, img, gain, shift)
-                else:
-                    normed, slope = NB[t, q, :], SB[t, q, :]
-                if t < 4:
-                    scaled = BK[px, :] * slope
-                    BK[px, :] = scaled
-                    if t in (0, 3):
-                        KB[t // 3, q, :] = slope
-                else:
-                    scaled = jnp.where(y > 0 if t == 4 else y < NY - 1, PB[t - 4, q, :] * slope, 0.0)
-                first[img] = first[img] + jnp.sum(scaled, axis=0, keepdims=True)
-                second[img] = second[img] + jnp.sum(scaled * normed, axis=0, keepdims=True)
-        value = jnp.zeros((8, 256), F32)
-        for img in range(2):
-            value = jnp.where(row8 == img, first[img], value)
-            value = jnp.where(row8 == 2 + img, second[img], value)
-        send_sums(n, value)
-        if n == 1:
-            spare_time()
-            ring_step(0, 0)
-        take_halo(n - 1, 1)
-        take_halo(n - 1, 0)
-        got = take_sums(n)
-        return got[0:2], got[2:4]
-
-    def norm_apply(a, t, img, first, second):
-        avg, inv = stats[a]
-        px = slice(t * PX + 64 * img, t * PX + 64 * img + 64)
-        v = Hx[a, t, 64 * img : 64 * img + 64, :]
-        i_ = inv[img : img + 1]
-        normed = (v - avg[img : img + 1]) * i_
-        return i_ * (BK[px, :] - first[img : img + 1] - normed * second[img : img + 1])
-
-    def spare_time():
-        pick = (iota((CH, 256), 0) == iota((CH, 256), 1) + BLK * x) & (iota((CH, 256), 1) < BLK)
-        pick = pick.astype(F32).astype(BF16)
-        for t in range(NX):
-            CC[t] = dot(G[t], pick)
+            v = Hx[a, t, q, :] if t < 4 else HxB[a, t - 4, q, :]
+            normed = (v - avg) * inv
+            linear = normed * gain + shift
+            s = jax.nn.sigmoid(linear)
+            NB[img, t] = normed
+            SB[img, t] = s * (1.0 + linear * (1.0 - s)) * gain
+
+    def norm_sums(n, img):
+        first = jnp.zeros((1, 256), F32)
+        second = jnp.zeros((1, 256), F32)
+        for t in range(6):
+            slope = SB[img, t]
+            if t < 4:
+                px = slice(64 * t, 64 * t + 64)
+                scaled = BK[img, px, :] * slope
+                BK[img, px, :] = scaled
+                if t in (0, 3):
+                    KB[img, t // 3] = slope
+            else:
+                valid = y > 0 if t == 4 else y < NY - 1
+                scaled = jnp.where(valid, PB[img, t - 4] * slope, 0.0)
+            first = first + jnp.sum(scaled, axis=0, keepdims=True)
+            second = second + jnp.sum(scaled * NB[img, t], axis=0, keepdims=True)
+        value = jnp.where(row8 == 0, first, jnp.where(row8 == 1, second, 0.0))
+        send_sums(2 * n + 1 + img, value)
+
+    def norm_finish(n, img):
+        take_halo(n, img, 1)
+        take_halo(n, img, 0)
+        got = take_sums(2 * n + 1 + img)
+        inv = stats[n][1][img : img + 1]
+        first, second = got[0:1], got[1:2]
+        return [
+            inv * (BK[img, 64 * t : 64 * t + 64, :] - first - NB[img, t] * second) for t in range(NX)
+        ]
 
     local_wait(G.at[0:3], rG)
     local_wait(W.at[1, 1 - c], rP.at[1])
-    conv(0, 1, mul_cot)
+    conv(0, 0, mul_cot)
     mean = take_sums(0)
     stats = []
     for a in range(2):
@@ -438,47 +429,58 @@
             HxB[a, e] = jnp.concatenate(
                 [both[:, BLK * a : BLK * a + BLK], jnp.zeros((PX, 256 - BLK), F32)], axis=1
             )
-    first, second = norm_sums(1, 0, params[0], params[1])
+    slopes(0, 0)
+    norm_sums(0, 0)
+    conv(0, 1, mul_cot)
+    slopes(0, 1)
+    norm_sums(0, 1)
+    ring_step(0, 0)
+    pick = (iota((CH, 256), 0) == iota((CH, 256), 1) + BLK * x) & (iota((CH, 256), 1) < BLK)
+    pick = pick.astype(F32).astype(BF16)
+    for t in range(NX):
+        CC[t] = dot(G[t], pick)
     for img in range(2):
         rest = jnp.zeros((64, 128), F32)
-        for t in range(NX):
-            v = norm_apply(0, t, img, first, second)
-            Gh[x, t * PX + 64 * img : t * PX + 64 * img + 64, :] = v[:, 0:128].astype(BF16)
+        for t, v in enumerate(norm_finish(0, img)):
+            Gh[img, x, 64 * t : 64 * t + 64, :] = v[:, 0:128].astype(BF16)
             rest = rest + (pltpu.roll(v[:, 128:256], 32 * t, 1) if t else v[:, 128:256])
-        Gh[x, 512 + 64 * img : 576 + 64 * img, :] = rest.astype(BF16)
-    for k in range(1, NX):
-        remote(Gh.at[x], Gh.at[x], sGh, rGh, dev(lax.rem(x + k, NX), y, z, c)).start()
+        Gh[img, x, 256:320, :] = rest.astype(BF16)
+        for k in range(1, NX):
+            remote(
+                Gh.at[img, x], Gh.at[img, x], sGh.at[img], rGh.at[img],
+                dev(lax.rem(x + k, NX), y, z, c),
+            ).start()
     for s in range(1, 4):
         ring_step(0, s)
     local_wait(W.at[0, 1 - c], rP.at[0])
     for k in range(NX):
         W1[:, :, 128 * k : 128 * k + 128, :] = W[0, :, :, BLK * k : BLK * k + 128, :]
         W1[:, :, 512 + 32 * k : 544 + 32 * k, :] = W[0, :, :, BLK * k + 128 : BLK * k + BLK, :]
-    for t in range(6):
-        for img in range(2):
-            q = slice(64 * img, 64 * img + 64)
-            NB[t, q, :], SB[t, q, :] = slopes(1, t, img, params[2], params[3])
-    local_wait(Gh.at[0:3], rGh)
-    lane = iota((PX, 128), 1)
-    rests = [Gh[k, 512:640, :].astype(F32) for k in range(NX)]
-    for k in range(NX):
-        L[:, 128 * k : 128 * k + 128] = Gh[k, 0:512, :]
-    for t in range(NX):
-        v = jnp.zeros((PX, 128), F32)
+    for img in range(2):
+        slopes(1, img)
+    lane = iota((64, 128), 1)
+    for img in range(2):
+        local_wait(Gh.at[img, 0:3], rGh.at[img])
+        rests = [Gh[img, k, 256:320, :].astype(F32) for k in range(NX)]
         for k in range(NX):
-            w = pltpu.roll(rests[k], (32 * (k - t)) % 128, 1) if k != t else rests[k]
-            v = jnp.where((lane >= 32 * k) & (lane < 32 * k + 32), w, v)
-        L[t * PX : t * PX + PX, 512:640] = v.astype(BF16)
-
-    conv(1, 0, mul_grad)
-    first, second = norm_sums(2, 1, params[2], params[3])
-    for t in range(NX):
-        v = jnp.concatenate([norm_apply(1, t, img, first, second) for img in range(2)], axis=0)
-        Os[t] = pack(CC[t] + v).astype(BF16)
-    for k in range(1, NX):
-        t = lax.rem(x + k, NX)
-        remote(Os.at[t], Oc.at[x], sO, rO, dev(t, y, z, c)).start()
-    Oc[x] = Os[x]
+            L[img, :, 128 * k : 128 * k + 128] = Gh[img, k, 0:256, :]
+        for t in range(NX):
+            v = jnp.zeros((64, 128), F32)
+            for k in range(NX):
+                w = pltpu.roll(rests[k], (32 * (k - t)) % 128, 1) if k != t else rests[k]
+                v = jnp.where((lane >= 32 * k) & (lane < 32 * k + 32), w, v)
+            L[img, 64 * t : 64 * t + 64, 512:640] = v.astype(BF16)
+        conv(1, img, mul_grad)
+        norm_sums(1, img)
+    for img in range(2):
+        for t, v in enumerate(norm_finish(1, img)):
+            Os[img, t] = pack(CC[t, 64 * img : 64 * img + 64, :] + v).astype(BF16)
+        for k in range(1, NX):
+            t = lax.rem(x + k, NX)
+            remote(
+                Os.at[img, t], Oc.at[img, x], sO.at[img], rO.at[img], dev(t, y, z, c)
+            ).start()
+        Oc[img, x] = Os[img, x]
 
     for f in (1, 0):
         local_wait(RA.at[f, 0:7], sA.at[f])
@@ -490,7 +492,8 @@
         local_wait(W.at[f, 0, :, 0:560, :], sR.at[f])
         local_wait(W.at[f, 0], sP.at[f])
     local_wait(G.at[0:3], sG)
-    local_wait(Gh.at[0:3], sGh)
+    for img in range(2):
+        local_wait(Gh.at[img, 0:3], sGh.at[img])
     local_wait(Hc.at[0:3], sH)
 
     @pl.when(y < NY - 1)
@@ -501,22 +504,24 @@
     def _():
         local_wait(Hc.at[0], sN.at[1])
 
-    for p in range(3):
+    for p in range(5):
         local_wait(ST.at[p, 0:7], sS.at[p])
-    for n in range(2):
+    for n, img in ((0, 0), (0, 1), (1, 0), (1, 1)):
         @pl.when(y > 0)
         def _():
-            local_wait(HBs.at[n, 0], sB.at[n, 0])
+            local_wait(HBs.at[n, img, 0], sB.at[n, img, 0])
 
         @pl.when(y < NY - 1)
         def _():
-            local_wait(HBs.at[n, 1], sB.at[n, 1])
-
-    local_wait(Oc.at[0:3], rO)
-    local_wait(Oc.at[0:3], sO)
-    out[...] = jnp.concatenate(
-        [unpack(Oc[k].astype(F32))[:, 0:BLK] for k in range(NX)], axis=1
-    ).astype(BF16)
+            local_wait(HBs.at[n, img, 1], sB.at[n, img, 1])
+
+    for img in range(2):
+        local_wait(Oc.at[img, 0:3], rO.at[img])
+        out[64 * img : 64 * img + 64, :] = jnp.concatenate(
+            [unpack(Oc[img, k].astype(F32))[:, 0:BLK] for k in range(NX)], axis=1
+        ).astype(BF16)
+    for img in range(2):
+        local_wait(Oc.at[img, 0:3], sO.at[img])
 
 
 def body(latent, hidden, cotangent, filter_one, filter_two, gain_one, shift_one, gain_two, shift_two):
@@ -540,34 +545,34 @@
             pltpu.VMEM((2, 3, CH, 256), BF16),
             pltpu.VMEM((2, 8, 24, 384), BF16),
             pltpu.VMEM((NX, PX, CH), BF16),
-            pltpu.VMEM((NX, 640, 128), BF16),
-            pltpu.VMEM((NX * PX, CH), BF16),
+            pltpu.VMEM((2, NX, 320, 128), BF16),
+            pltpu.VMEM((2, NX * 64, CH), BF16),
             pltpu.VMEM((NX, PX, 384), BF16),
             pltpu.VMEM((NX, PX, 384), BF16),
             pltpu.VMEM((2, NX, PX, 256), F32),
-            pltpu.VMEM((3, 8, 128), F32),
-            pltpu.VMEM((3, NY, 8, 128), F32),
+            pltpu.VMEM((5, 8, 128), F32),
+            pltpu.VMEM((5, NY, 8, 128), F32),
             pltpu.VMEM((2, PX, 384), BF16),
             pltpu.VMEM((2, 2, PX, 256), F32),
-            pltpu.VMEM((6, PX, 256), F32),
-            pltpu.VMEM((6, PX, 256), F32),
-            pltpu.VMEM((2, PX, 256), F32),
-            pltpu.VMEM((2, PX, 256), F32),
-            pltpu.VMEM((2, 2, BLK, 128), F32),
-            pltpu.VMEM((2, 2, BLK, 128), F32),
-            pltpu.VMEM((2, NX * PX, 256), F32),
-            pltpu.VMEM((NX * PX, 256), F32),
-            pltpu.VMEM((NX, BLK, 128), BF16),
-            pltpu.VMEM((NX, BLK, 128), BF16),
+            pltpu.VMEM((2, 6, 64, 256), F32),
+            pltpu.VMEM((2, 6, 64, 256), F32),
+            pltpu.VMEM((2, 2, 64, 256), F32),
+            pltpu.VMEM((2, 2, 64, 256), F32),
+            pltpu.VMEM((2, 2, 2, 80, 128), F32),
+            pltpu.VMEM((2, 2, 2, 80, 128), F32),
+            pltpu.VMEM((2, NX * 64, 256), F32),
+            pltpu.VMEM((2, NX * 64, 256), F32),
+            pltpu.VMEM((2, NX, 80, 128), BF16),
+            pltpu.VMEM((2, NX, 80, 128), BF16),
             pltpu.VMEM((NX, PX, 256), F32),
             dma((2,)), dma((4,)), dma((2,)), dma,
             dma((2,)), dma((2,)), dma((2,)),
             dma((2,)), dma((2, 2, 4, 3)),
             dma((2,)), dma((2,)),
-            dma, dma, dma, dma, dma, dma,
-            dma((3,)), dma((3,)),
-            dma((2, 2)), dma((2, 2)),
-            dma, dma,
+            dma, dma, dma((2,)), dma((2,)), dma, dma,
+            dma((5,)), dma((5,)),
+            dma((2, 2, 2)), dma((2, 2, 2)),
+            dma((2,)), dma((2,)),
             dma((2,)), dma((2,)),
         ],
         compiler_params=pltpu.CompilerParams(

time: 68.8 us -> 67.2 us (0.977)
  Pallas kernels: 67 us -> 65.5 us
    pallas_call x1, Pallas kernels: 67 us -> 65.5 us  [body(): pl.pallas_call(kernel, out_shape=jax.ShapeDtypeStruct((PX, CH), BF16), in...]
where the time goes in v6:
time: 67.2 us; the launch traced here: 67.1 us
  Pallas kernels  65.5 us (97%)
  local copies, waits for them, and re-layouts  1.6 us (2%)
    pallas_call x1, Pallas kernels, body(): pl.pallas_call(kernel, out_shape=jax.ShapeDtypeStruct((PX, CH), BF16), in...  65.5 us
    unnamed x1, local copies, waits for them, and re-layouts  1.6 us

profile of v6, /device:TPU:1, one launch (start us, length us, event | category | flops | bytes accessed | tf_op | source)
XLA Modules:
  0.0 67.1 jit_solution(1573246619785360579)
XLA Ops:
  0.0 65.5 %block_backward.1 = bf16[128,640]{1,0:T(8,128)(2,1)} custom-call(bf16[9,20,40]{2,1,0:T(8,128)(2,1)} %bitcast.12, bf16[9,20,40]{2,1,0:T(8,128)(2,1)} %bitcast.13, bf16[128,640]{1,0:T(8,128)(2,1)} %bitcast.9, bf16[128,640]{1,0:T(8,128)(2,1)} %bitcast.10, bf16[128,640]{1,0:T(8,128)(2,1)} %bitcast.11, f32[640]{0:T(1024)} %g2.1, f32[640]{0:T(1024)} %s2_.1, ...), custom_call_target="tpu_custom_call" | custom-call | tf_op jit(solution)/shard_map/block_backward/pallas_call | solution.py:534
  65.5 1.6 %copy.12 = bf16[2,1,64,640]{3,2,1,0:T(8,128)(2,1)} copy(bf16[2,1,64,640]{3,2,1,0:T(8,128)(2,1)} %bitcast.8) | data formatting | bytes 327680

commit v7 on v6

--- a/solution.py
+++ b/solution.py
@@ -13,6 +13,7 @@
 BLK = 160
 PX = 128
 NUMBER = 32 * 64 * 40
+FAR_FIRST = (4, 3, 5, 2, 6, 1, 7)
 
 
 def dev(x, y, z, c):
@@ -118,7 +119,7 @@
     place = {f: jnp.where(along_y[f], y, z) for f in (1, 0)}
 
     def first_stage(f):
-        for k in range(8):
+        for k in FAR_FIRST + (0,):
             y_ = jnp.where(along_y[f], y, lax.rem(y + k, NY))
             z_ = jnp.where(along_y[f], lax.rem(z + k, NZ), y)
             target = dev(X, y_, z_, c)
@@ -229,14 +230,6 @@
 
     row8 = iota((8, 256), 0)
     local_wait(Hc.at[0:3], rH)
-    @pl.when(y < NY - 1)
-    def _():
-        remote(Hc.at[3], Hb.at[0], sN.at[0], rN.at[0], dev(x, lax.rem(y + 1, 8), z, c)).start()
-
-    @pl.when(y > 0)
-    def _():
-        remote(Hc.at[0], Hb.at[1], sN.at[1], rN.at[1], dev(x, lax.rem(y + 7, 8), z, c)).start()
-
     zero = jnp.zeros((64, 256 - BLK), F32)
     sums = jnp.zeros((8, 256), F32)
     for img in range(2):
@@ -270,7 +263,7 @@
         value = group_totals(value)
         SS[p] = value
         ST[p, y] = value
-        for k in range(1, NY):
+        for k in FAR_FIRST:
             remote(
                 SS.at[p], ST.at[p, y], sS.at[p], rS.at[p], dev(x, lax.rem(y + k, NY), z, c)
             ).start()
@@ -285,9 +278,17 @@
         return jnp.concatenate([tot, last], axis=1)
 
     send_sums(0, sums)
-    for s in range(2, 4):
-        ring_step(1, s)
+    @pl.when(y < NY - 1)
+    def _():
+        remote(Hc.at[3], Hb.at[0], sN.at[0], rN.at[0], dev(x, lax.rem(y + 1, 8), z, c)).start()
+
+    @pl.when(y > 0)
+    def _():
+        remote(Hc.at[0], Hb.at[1], sN.at[1], rN.at[1], dev(x, lax.rem(y + 7, 8), z, c)).start()
+
+    ring_step(1, 2)
     start_ring(0)
+    ring_step(1, 3)
 
     ln128 = iota((16, 128), 1)
 
@@ -445,7 +446,7 @@
             Gh[img, x, 64 * t : 64 * t + 64, :] = v[:, 0:128].astype(BF16)
             rest = rest + (pltpu.roll(v[:, 128:256], 32 * t, 1) if t else v[:, 128:256])
         Gh[img, x, 256:320, :] = rest.astype(BF16)
-        for k in range(1, NX):
+        for k in (2, 1, 3):
             remote(
                 Gh.at[img, x], Gh.at[img, x], sGh.at[img], rGh.at[img],
                 dev(lax.rem(x + k, NX), y, z, c),
@@ -475,7 +476,7 @@
     for img in range(2):
         for t, v in enumerate(norm_finish(1, img)):
             Os[img, t] = pack(CC[t, 64 * img : 64 * img + 64, :] + v).astype(BF16)
-        for k in range(1, NX):
+        for k in (2, 1, 3):
             t = lax.rem(x + k, NX)
             remote(
                 Os.at[img, t], Oc.at[img, x], sO.at[img], rO.at[img], dev(t, y, z, c)

time: 67.2 us -> 66 us (0.982)
  Pallas kernels: 65.5 us -> 64.3 us
    pallas_call x1, Pallas kernels: 65.5 us -> 64.3 us  [body(): pl.pallas_call(kernel, out_shape=jax.ShapeDtypeStruct((PX, CH), BF16), in...]
where the time goes in v7:
time: 66 us; the launch traced here: 65.9 us
  Pallas kernels  64.3 us (97%)
  local copies, waits for them, and re-layouts  1.6 us (2%)
    pallas_call x1, Pallas kernels, body(): pl.pallas_call(kernel, out_shape=jax.ShapeDtypeStruct((PX, CH), BF16), in...  64.3 us
    unnamed x1, local copies, waits for them, and re-layouts  1.6 us

profile of v7, /device:TPU:1, one launch (start us, length us, event | category | flops | bytes accessed | tf_op | source)
XLA Modules:
  0.0 65.9 jit_solution(10153592866426412011)
XLA Ops:
  0.0 64.3 %block_backward.1 = bf16[128,640]{1,0:T(8,128)(2,1)} custom-call(bf16[9,20,40]{2,1,0:T(8,128)(2,1)} %bitcast.12, bf16[9,20,40]{2,1,0:T(8,128)(2,1)} %bitcast.13, bf16[128,640]{1,0:T(8,128)(2,1)} %bitcast.9, bf16[128,640]{1,0:T(8,128)(2,1)} %bitcast.10, bf16[128,640]{1,0:T(8,128)(2,1)} %bitcast.11, f32[640]{0:T(1024)} %g2.1, f32[640]{0:T(1024)} %s2_.1, ...), custom_call_target="tpu_custom_call" | custom-call | tf_op jit(solution)/shard_map/block_backward/pallas_call | solution.py:535
  64.3 1.6 %copy.12 = bf16[2,1,64,640]{3,2,1,0:T(8,128)(2,1)} copy(bf16[2,1,64,640]{3,2,1,0:T(8,128)(2,1)} %bitcast.8) | data formatting | bytes 327680

commit v8 on v7

--- a/solution.py
+++ b/solution.py
@@ -287,8 +287,16 @@
         remote(Hc.at[0], Hb.at[1], sN.at[1], rN.at[1], dev(x, lax.rem(y + 7, 8), z, c)).start()
 
     ring_step(1, 2)
-    start_ring(0)
+    @pl.when(c == 1)
+    def _():
+        start_ring(0)
+
     ring_step(1, 3)
+
+    @pl.when(c == 0)
+    def _():
+        start_ring(0)
+
 
     ln128 = iota((16, 128), 1)
 
@@ -330,14 +338,17 @@
 
     def conv(n, img, mul):
         for cc in range(2):
-            AC[cc] = mul(img, cc, 1, 0, 4)
-            AC[cc, 0:192] += mul(img, cc, 0, 1, 4)
-            AC[cc, 64:256] += mul(img, cc, 2, 0, 3)
-        BK[img] = combine([AC[0], AC[1]])
-        for e, (ai, t) in enumerate(((0, 0), (2, 3))):
-            PB[img, e] = combine([mul(img, cc, ai, t, t + 1) for cc in range(2)])
-            HBs[n, img, e] = pack(PB[img, e])
-
+            AC[cc, 256:384] = jnp.zeros((128, 256), F32)
+            AC[cc, 0:256] = mul(img, cc, 0)
+            AC[cc, 64:320] += mul(img, cc, 1)
+            AC[cc, 128:384] += mul(img, cc, 2)
+        back = combine([AC[0], AC[1]])
+        BK[img] = back[64:320]
+        for e in range(2):
+            PB[img, e] = back[320 * e : 320 * e + 64]
+            HBs[n, img, e] = pack(back[320 * e : 320 * e + 64])
+
+    def send_halo(n, img):
         @pl.when(y > 0)
         def _():
             remote(
@@ -359,12 +370,11 @@
             px = slice(192, 256) if e == 0 else slice(0, 64)
             BK[img, px] += unpack(HBr[n, img, e]) * KB[img, 1 - e]
 
-    def mul_cot(img, cc, ai, t0, t1):
-        rows = G[t0:t1, 64 * img : 64 * img + 64, :].reshape((t1 - t0) * 64, CH)
-        return dot(rows, W[1, cc, ai])
-
-    def mul_grad(img, cc, ai, t0, t1):
-        return dot(L[img, 64 * t0 : 64 * t1, :], W1[cc, ai])
+    def mul_cot(img, cc, ai):
+        return dot(G[:, 64 * img : 64 * img + 64, :].reshape(NX * 64, CH), W[1, cc, ai])
+
+    def mul_grad(img, cc, ai):
+        return dot(L[img], W1[cc, ai])
 
     def slopes(a, img):
         avg, inv = (v[img : img + 1] for v in stats[a])
@@ -396,6 +406,7 @@
             second = second + jnp.sum(scaled * NB[img, t], axis=0, keepdims=True)
         value = jnp.where(row8 == 0, first, jnp.where(row8 == 1, second, 0.0))
         send_sums(2 * n + 1 + img, value)
+        send_halo(n, img)
 
     def norm_finish(n, img):
         take_halo(n, img, 1)
@@ -432,8 +443,8 @@
             )
     slopes(0, 0)
     norm_sums(0, 0)
+    slopes(0, 1)
     conv(0, 1, mul_cot)
-    slopes(0, 1)
     norm_sums(0, 1)
     ring_step(0, 0)
     pick = (iota((CH, 256), 0) == iota((CH, 256), 1) + BLK * x) & (iota((CH, 256), 1) < BLK)
@@ -561,7 +572,7 @@
             pltpu.VMEM((2, 2, 64, 256), F32),
             pltpu.VMEM((2, 2, 2, 80, 128), F32),
             pltpu.VMEM((2, 2, 2, 80, 128), F32),
-            pltpu.VMEM((2, NX * 64, 256), F32),
+            pltpu.VMEM((2, 384, 256), F32),
             pltpu.VMEM((2, NX * 64, 256), F32),
             pltpu.VMEM((2, NX, 80, 128), BF16),
             pltpu.VMEM((2, NX, 80, 128), BF16),

time: 66 us -> 65.3 us (0.989)
  Pallas kernels: 64.3 us -> 63.5 us
    pallas_call x1, Pallas kernels: 64.3 us -> 63.5 us  [body(): pl.pallas_call(kernel, out_shape=jax.ShapeDtypeStruct((PX, CH), BF16), in...]
where the time goes in v8:
time: 65.3 us; the launch traced here: 65.1 us
  Pallas kernels  63.5 us (97%)
  local copies, waits for them, and re-layouts  1.6 us (2%)
    pallas_call x1, Pallas kernels, body(): pl.pallas_call(kernel, out_shape=jax.ShapeDtypeStruct((PX, CH), BF16), in...  63.5 us
    unnamed x1, local copies, waits for them, and re-layouts  1.6 us

profile of v8, /device:TPU:1, one launch (start us, length us, event | category | flops | bytes accessed | tf_op | source)
XLA Modules:
  0.0 65.1 jit_solution(17060739933329153872)
XLA Ops:
  0.0 63.5 %block_backward.1 = bf16[128,640]{1,0:T(8,128)(2,1)} custom-call(bf16[9,20,40]{2,1,0:T(8,128)(2,1)} %bitcast.12, bf16[9,20,40]{2,1,0:T(8,128)(2,1)} %bitcast.13, bf16[128,640]{1,0:T(8,128)(2,1)} %bitcast.9, bf16[128,640]{1,0:T(8,128)(2,1)} %bitcast.10, bf16[128,640]{1,0:T(8,128)(2,1)} %bitcast.11, f32[640]{0:T(1024)} %g2.1, f32[640]{0:T(1024)} %s2_.1, ...), custom_call_target="tpu_custom_call" | custom-call | tf_op jit(solution)/shard_map/block_backward/pallas_call | solution.py:546
  63.5 1.6 %copy.12 = bf16[2,1,64,640]{3,2,1,0:T(8,128)(2,1)} copy(bf16[2,1,64,640]{3,2,1,0:T(8,128)(2,1)} %bitcast.8) | data formatting | bytes 327680

commit v9 on v8

--- a/solution.py
+++ b/solution.py
@@ -144,12 +144,9 @@
             axis=1,
         ).astype(BF16)
     own_cot.wait()
-    for k in range(1, NX):
+    for k in (2, 1, 3):
         t = lax.rem(x + k, NX)
         remote(Hs.at[t], Hc.at[x], sH, rH, dev(t, y, z, c)).start()
-    for k in range(1, NX):
-        t = lax.rem(x + k, NX)
-        remote(G.at[x], G.at[x], sG, rG, dev(t, y, z, c)).start()
     Hc[x] = Hs[x]
     own_block(0)
     params = []
@@ -224,6 +221,9 @@
                 share(f, a, place[f] - (step + 1) * (1 if way == 0 else -1))
 
     start_ring(1)
+    for k in (2, 1, 3):
+        t = lax.rem(x + k, NX)
+        remote(G.at[x], G.at[x], sG, rG, dev(t, y, z, c)).start()
     first_stage(0)
     for s in range(2):
         ring_step(1, s)

time: 65.3 us -> 65.1 us (level)
  no operation moved by 1% of the time
where the time goes in v9:
time: 65.1 us; the launch traced here: 65 us
  Pallas kernels  63.4 us (97%)
  local copies, waits for them, and re-layouts  1.6 us (2%)
    pallas_call x1, Pallas kernels, body(): pl.pallas_call(kernel, out_shape=jax.ShapeDtypeStruct((PX, CH), BF16), in...  63.4 us
    unnamed x1, local copies, waits for them, and re-layouts  1.6 us

profile of v9, /device:TPU:1, one launch (start us, length us, event | category | flops | bytes accessed | tf_op | source)
XLA Modules:
  0.0 65.0 jit_solution(4124846112146537253)
XLA Ops:
  0.0 63.4 %block_backward.1 = bf16[128,640]{1,0:T(8,128)(2,1)} custom-call(bf16[9,20,40]{2,1,0:T(8,128)(2,1)} %bitcast.12, bf16[9,20,40]{2,1,0:T(8,128)(2,1)} %bitcast.13, bf16[128,640]{1,0:T(8,128)(2,1)} %bitcast.9, bf16[128,640]{1,0:T(8,128)(2,1)} %bitcast.10, bf16[128,640]{1,0:T(8,128)(2,1)} %bitcast.11, f32[640]{0:T(1024)} %g2.1, f32[640]{0:T(1024)} %s2_.1, ...), custom_call_target="tpu_custom_call" | custom-call | tf_op jit(solution)/shard_map/block_backward/pallas_call | solution.py:546
  63.4 1.6 %copy.12 = bf16[2,1,64,640]{3,2,1,0:T(8,128)(2,1)} copy(bf16[2,1,64,640]{3,2,1,0:T(8,128)(2,1)} %bitcast.8) | data formatting | bytes 327680

commit v10 on v8

--- a/solution.py
+++ b/solution.py
@@ -38,7 +38,7 @@
 def kernel(
     f1, f2, cot, hid, lat, g2, s2, g1, s1, out,
     FV, PV, HV, WB, W, W1, RA, G, Gh, L, Hs, Hc, Hx, SS, ST, Hb, HxB, NB, SB, PB, KB, HBs, HBr, AC, BK, Os, Oc, CC,
-    lF, lP, lH, lC, sA, sA0, rA, sR, rR, sP, rP, sG, rG, sGh, rGh, sH, rH, sS, rS, sB, rB, sO, rO, sN, rN,
+    lF, lP, lH, lC, sA, sA0, rA, sR, rR, sP, rP, sG, rG, sGh, rGh, sH, rH, sS, rS, sB, rB, sO, rO, sN, rN, OV, sV,
 ):
     dp = lax.axis_index("dp")
     rr = lax.axis_index("rows")
@@ -529,11 +529,13 @@
 
     for img in range(2):
         local_wait(Oc.at[img, 0:3], rO.at[img])
-        out[64 * img : 64 * img + 64, :] = jnp.concatenate(
+        OV[64 * img : 64 * img + 64, :] = jnp.concatenate(
             [unpack(Oc[img, k].astype(F32))[:, 0:BLK] for k in range(NX)], axis=1
         ).astype(BF16)
+        pltpu.make_async_copy(OV.at[pl.ds(64 * img, 64), :], out.at[pl.ds(64 * img, 64), :], sV.at[img]).start()
     for img in range(2):
         local_wait(Oc.at[img, 0:3], sO.at[img])
+        local_wait(OV.at[pl.ds(64 * img, 64), :], sV.at[img])
 
 
 def body(latent, hidden, cotangent, filter_one, filter_two, gain_one, shift_one, gain_two, shift_two):
@@ -547,7 +549,7 @@
         kernel,
         out_shape=jax.ShapeDtypeStruct((PX, CH), BF16),
         in_specs=[anywhere] * 9,
-        out_specs=vmem,
+        out_specs=pl.BlockSpec(memory_space=pltpu.HBM),
         scratch_shapes=[
             pltpu.VMEM((2, 9, 20, 40), BF16),
             [pltpu.VMEM((CH,), F32)] * 4,
@@ -586,6 +588,7 @@
             dma((2, 2, 2)), dma((2, 2, 2)),
             dma((2,)), dma((2,)),
             dma((2,)), dma((2,)),
+            pltpu.VMEM((PX, CH), BF16), dma((2,)),
         ],
         compiler_params=pltpu.CompilerParams(
             collective_id=0, has_side_effects=True, vmem_limit_bytes=62 * 1024 * 1024

time: 65.3 us -> 65.3 us (level)
  no operation moved by 1% of the time
where the time goes in v10:
time: 65.3 us; the launch traced here: 65.1 us
  Pallas kernels  63.5 us (97%)
  local copies, waits for them, and re-layouts  1.6 us (2%)
    pallas_call x1, Pallas kernels, body(): pl.pallas_call(kernel, out_shape=jax.ShapeDtypeStruct((PX, CH), BF16), in...  63.5 us
    unnamed x1, local copies, waits for them, and re-layouts  1.6 us

profile of v10, /device:TPU:1, one launch (start us, length us, event | category | flops | bytes accessed | tf_op | source)
XLA Modules:
  0.0 65.1 jit_solution(10417252909166616987)
XLA Ops:
  0.0 63.5 %block_backward.1 = bf16[128,640]{1,0:T(8,128)(2,1)} custom-call(bf16[9,20,40]{2,1,0:T(8,128)(2,1)} %bitcast.12, bf16[9,20,40]{2,1,0:T(8,128)(2,1)} %bitcast.13, bf16[128,640]{1,0:T(8,128)(2,1)} %bitcast.9, bf16[128,640]{1,0:T(8,128)(2,1)} %bitcast.10, bf16[128,640]{1,0:T(8,128)(2,1)} %bitcast.11, f32[640]{0:T(1024)} %g2.1, f32[640]{0:T(1024)} %s2_.1, ...), custom_call_target="tpu_custom_call" | custom-call | tf_op jit(solution)/shard_map/block_backward/pallas_call | solution.py:548
  63.5 1.6 %copy.12 = bf16[2,1,64,640]{3,2,1,0:T(8,128)(2,1)} copy(bf16[2,1,64,640]{3,2,1,0:T(8,128)(2,1)} %bitcast.8) | data formatting | bytes 327680
